TPU v7x, 128 devices: a whole 4x4x4 slice. The times are simulated.
128 devices in a mesh: gx: 4 (over y), gy: 8 (over x, core), gz: 4 (over z).
Axes of the slice: x: 4, y: 4, z: 4, core: 2. Of those that a mesh axis runs over, the one named last changes fastest.
Arguments:
- rhs: float32 [8, 64, 256, 512], P(None, 'gx', 'gy', 'gz'), may hold values from -8 to 8
- stencil: float32 [14, 64, 256, 512], P(None, 'gx', 'gy', 'gz'), may hold values from 0.02 to 1
Outputs:
- solution: float32 [8, 64, 256, 512], P(None, 'gx', 'gy', 'gz')
- residual: float32 [8, 64, 256, 512], P(None, 'gx', 'gy', 'gz')
All inputs are finite; a program needn't handle non-finite values.
Results may differ from a plain program's by a relative error of at most 0.00029.
Values sent between devices are 32-bit elements; how exact they have to be, the bound alone decides.
A program may use at most 128 MiB of HBM per device.

v0:
```python
import jax
import jax.numpy as jnp
from jax import lax
from jax.sharding import Mesh
from jax.sharding import PartitionSpec as P

ITERS = 2
GX_GY_GZ = ("gx", "gy_0", "gy_1", "gz")
GY = ("gy_0", "gy_1")


FORWARD = [
    (a, b, c) for a in (-1, 0, 1) for b in (-1, 0, 1) for c in (-1, 0, 1) if (a, b, c) > (0, 0, 0)
]


def over_axes(x, axes):
    for axis in axes:
        x = lax.psum(x, axis)
    return x


def with_halo(cells, sides, width):
    for axis, dim in sides:
        count = lax.axis_size(axis)
        ends = count - 1
        head = lax.slice_in_dim(cells, 0, width, axis=dim)
        tail = lax.slice_in_dim(cells, cells.shape[dim] - width, cells.shape[dim], axis=dim)
        cells = jnp.concatenate(
            [
                lax.ppermute(tail, axis, [(i, (i + 1) % count) for i in range(ends)]),
                cells,
                lax.ppermute(head, axis, [((i + 1) % count, i) for i in range(ends)]),
            ],
            axis=dim,
        )
    return cells


def window(array, margin, depth, offset):
    result = array
    for place in range(3):
        dim = array.ndim - 3 + place
        inner = array.shape[dim] - 2 * margin
        begin = margin - depth + offset[place]
        result = lax.slice_in_dim(result, begin, begin + inner + 2 * depth, axis=dim)
    return result


def diagonal_field(padded, margin, depth):
    total = window(padded[0], margin, depth, (0, 0, 0))
    total = total + jnp.sum(window(padded[1:], margin, depth, (0, 0, 0)), axis=0)
    for index, offset in enumerate(FORWARD):
        back = (-offset[0], -offset[1], -offset[2])
        total = total + window(padded[index + 1], margin, depth, back)
    return total


def operate(field, fmargin, padded, smargin, diag, depth):
    result = diag[None] * window(field, fmargin, depth, (0, 0, 0))
    for index, offset in enumerate(FORWARD):
        back = (-offset[0], -offset[1], -offset[2])
        ahead_w = window(padded[index + 1], smargin, depth, (0, 0, 0))
        behind_w = window(padded[index + 1], smargin, depth, back)
        result = result - ahead_w[None] * window(field, fmargin, depth, offset)
        result = result - behind_w[None] * window(field, fmargin, depth, back)
    return result


def gram(left, right):
    flat_l = left.reshape(left.shape[0], -1)
    flat_r = right.reshape(right.shape[0], -1)
    return lax.dot_general(
        flat_l,
        flat_r,
        (((1,), (1,)), ((), ())),
        precision=lax.Precision.HIGHEST,
        preferred_element_type=jnp.float32,
    )


def combine(coef, field):
    return jnp.einsum("ij,ixyz->jxyz", coef, field, precision=lax.Precision.HIGHEST)


def small_dot(left, right):
    return jnp.dot(left, right, precision=lax.Precision.HIGHEST)


def solve_spd(matrix, right):
    factor = jnp.linalg.cholesky(matrix)
    return jax.scipy.linalg.cho_solve((factor, True), right)


def joint_sum(residual, direction, image):
    parts = (
        gram(residual, residual),
        gram(direction, image),
        gram(image, residual),
        gram(image, image),
    )
    return (
        over_axes(parts[0], GX_GY_GZ),
        over_axes(parts[1], GX_GY_GZ),
        over_axes(parts[2], GX_GY_GZ),
        over_axes(parts[3], GX_GY_GZ),
    )


def shards(rhs, stencil):
    padded = with_halo(stencil, (("gx", 1), (GY, 2), ("gz", 3)), 1)
    smargin = 1
    diag_full = diagonal_field(padded, 1, 0)
    direction = rhs
    dmargin = 0
    residual = direction
    rmargin = dmargin
    solution = jnp.zeros_like(rhs)
    norm_now = None
    for step in range(ITERS):
        field = with_halo(direction, (("gx", 1), (GY, 2), ("gz", 3)), 1)
        fmargin = 1
        depth = 0
        image = operate(field, fmargin, padded, smargin, diag_full, depth)
        dir_here = window(field, fmargin, depth, (0, 0, 0))
        res_here = window(residual, rmargin, depth, (0, 0, 0))
        dir_core = window(dir_here, depth, 0, (0, 0, 0))
        res_core = window(res_here, depth, 0, (0, 0, 0))
        img_core = window(image, depth, 0, (0, 0, 0))
        norm_now, curve, cross, square = joint_sum(res_core, dir_core, img_core)
        alpha = solve_spd(curve, norm_now)
        solution = solution + combine(alpha, dir_core)
        res_here = res_here - combine(alpha, image)
        if step + 1 < ITERS:
            norm_next = (
                norm_now
                - small_dot(alpha.T, cross)
                - small_dot(cross.T, alpha)
                + small_dot(alpha.T, small_dot(square, alpha))
            )
            beta = solve_spd(norm_now, norm_next)
            direction = res_here + combine(beta, dir_here)
            norm_now = norm_next
        residual = res_here
        rmargin = depth
    return (solution, window(residual, rmargin, 0, (0, 0, 0)))


def solution(mesh):
    split = Mesh(
        mesh.devices.reshape(mesh.shape["gx"], 4, 2, mesh.shape["gz"]), ("gx", "gy_0", "gy_1", "gz")
    )
    placed = (P(None, "gx", GY, "gz"), P(None, "gx", GY, "gz"))
    return jax.shard_map(
        shards,
        mesh=split,
        in_specs=placed,
        out_specs=(P(None, "gx", GY, "gz"), P(None, "gx", GY, "gz")),
        check_vma=False,
    )
```

profile of v0, /device:TPU:1, one launch (start us, length us, event | category | flops | bytes accessed | tf_op | source)
XLA Modules:
  0.0 388.8 jit_solution(6726327322583336218)
XLA Ops:
  0.6 3.4 copy.170
  4.1 4.0 %collective-permute-start.6 = (f32[8,1,32,128]{3,0,2,1:T(8,128)S(1)}, f32[8,1,32,128]{3,0,2,1:T(8,128)S(1)}, u32[]{:S(2)}, u32[]{:S(2)}) collective-permute-start(f32[8,1,32,128]{3,0,2,1:T(8,128)S(1)} %get-tuple-element.82), channel_id=1, source_target_pairs={{0,32},{32,64},{64,96},{1,33},{33,65},{65,97},{2,34},{34,66},{66,9... | collective-permute-start | bytes 393224 | tf_op jit(solution)/shard_map/ppermute | solution.py:31
  9.2 3.2 collective-permute-start
  15.7 1.7 constant_dynamic-update-slice_fusion.4
  17.4 5.6 %collective-permute-done.7 = f32[8,1,32,128]{3,0,2,1:T(8,128)S(1)} collective-permute-done((f32[8,1,32,128]{3,0,2,1:T(8,128)S(1)}, f32[8,1,32,128]{3,0,2,1:T(8,128)S(1)}, u32[]{:S(2)}, u32[]{:S(2)}) %collective-permute-start.7) | collective-permute-done | bytes 131104 | tf_op jit(solution)/shard_map/ppermute | solution.py:33
  23.1 5.1 %collective-permute-start.8 = (f32[8,18,1,128]{3,0,2,1:T(8,128)S(1)}, f32[8,18,1,128]{3,0,2,1:T(8,128)S(1)}, u32[]{:S(2)}, u32[]{:S(2)}) collective-permute-start(f32[8,18,1,128]{3,0,2,1:T(8,128)S(1)} %get-tuple-element.78), channel_id=1, source_target_pairs={{0,4},{4,8},{8,12},{12,16},{16,20},{20,24},{24,28},{1,5},{5,9},{9,... | collective-permute-start | bytes 221192 | tf_op jit(solution)/shard_map/ppermute | solution.py:31
  28.2 1.9 collective-permute-start.9
  31.2 2.6 collective-permute-done.9
  34.0 3.0 fusion.107
  37.0 2.8 copy.174
  41.1 2.8 copy.176
  43.9 4.2 %collective-permute-start.11 = (f32[8,18,34,1]{2,0,3,1:T(8,128)S(1)}, f32[8,18,34,1]{2,0,3,1:T(8,128)S(1)}, u32[]{:S(2)}, u32[]{:S(2)}) collective-permute-start(f32[8,18,34,1]{2,0,3,1:T(8,128)S(1)} %copy.176), channel_id=1, source_target_pairs={{0,1},{1,2},{2,3},{4,5},{5,6},{6,7},{8,9},{9,10},{10,11},{12,13},{... | collective-permute-start | bytes 58760 | tf_op jit(solution)/shard_map/ppermute | solution.py:31
  48.1 2.5 constant_dynamic-update-slice_fusion.1
  50.7 1.9 copy-done.5
  52.8 2.2 collective-permute-start.2
  55.1 2.4 collective-permute-start.3
  57.5 5.5 %convolution_bitcast_fusion.5 = f32[8,8]{0,1:T(8,128)} fusion(f32[8,16,32,128]{3,2,1,0:T(8,128)S(1)} %copy-done), kind=kOutput, calls=%fused_computation.145 | convolution fusion | flops 50331648 | bytes 2097408 | tf_op jit(solution)/shard_map/dot_general | solution.py:73
  63.0 2.6 copy.175
  65.6 2.6 copy.177
  68.5 2.8 pad_maximum_fusion.1
  71.3 5.6 %fusion.103 = (f32[14,18,34,1]{3,2,1,0:T(8,128)}, f32[14,18,34,1]{3,2,1,0:T(8,128)}) fusion(f32[14,18,34,128]{3,2,1,0:T(8,128)S(1)} %pad_maximum_fusion.1), kind=kLoop, calls=%fused_computation.230 | loop fusion | bytes 137088 | tf_op jit(solution)/shard_map/slice | solution.py:28
  76.9 3.9 %copy.164 = f32[14,18,34,1]{2,0,3,1:T(8,128)S(1)} copy(f32[14,18,34,1]{3,2,1,0:T(8,128)} %get-tuple-element.59) | data formatting | bytes 68544 | tf_op jit(solution)/shard_map/slice | solution.py:28
  80.8 3.6 collective-permute-start.4
  84.4 3.9 %copy.165 = f32[14,18,34,1]{2,0,3,1:T(8,128)S(1)} copy(f32[14,18,34,1]{3,2,1,0:T(8,128)} %get-tuple-element.60) | data formatting | bytes 68544 | tf_op jit(solution)/shard_map/slice | solution.py:27
  88.3 1.8 collective-permute-start.5
  90.2 7.9 %pad_maximum_fusion.2 = (f32[8,18,34,129]{3,0,2,1:T(8,128)}, f32[8,18,34,129]{3,0,2,1:T(8,128)}) fusion(f32[8,18,34,1]{3,0,2,1:T(8,128)} %copy.175, f32[8,18,1,128]{3,0,2,1:T(8,128)S(1)} %collective-permute-done.9, f32[8,18,32,128]{3,0,2,1:T(8,128)} %copy-done.4, f32[8,18,1,128]{3,0,2,1:T(8,128)S(1)} %collective-permute-done.8, f32[8,18,34,1]{3,0,2,1:T(8,128)} %copy.177), kind=kLoop, calls=%fused_computation.2 | loop fusion | flops 3789504 | bytes 7598592 | tf_op jit(solution)/shard_map/concatenate | solution.py:29
  98.1 3.5 copy.166
  101.6 3.5 copy.167
  105.1 13.4 %pad_maximum_fusion = f32[14,18,34,130]{3,2,1,0:T(8,128)} fusion(f32[14,18,34,1]{3,2,1,0:T(8,128)} %copy.167, f32[14,18,1,128]{3,2,1,0:T(1,128)S(1)} %copy.163, f32[14,18,32,128]{3,2,1,0:T(8,128)} %copy-done.5, f32[14,18,1,128]{3,2,1,0:T(1,128)S(1)} %copy.162, f32[14,18,34,1]{3,2,1,0:T(8,128)} %copy.166), kind=kLoop, calls=%fused_computation | loop fusion | flops 4455360 | bytes 8910720 | tf_op jit(solution)/shard_map/concatenate | solution.py:29
  118.5 8.0 %slice_bitcast_fusion.13 = (f32[16,34,130]{2,1,0:T(8,128)}, f32[1,16,34,130]{3,2,1,0:T(8,128)S(1)}, f32[1,16,34,130]{3,2,1,0:T(8,128)S(1)}, f32[1,16,34,130]{3,2...) fusion(f32[14,18,34,130]{3,2,1,0:T(8,128)} %pad_maximum_fusion), kind=kLoop, calls=%fused_computation.159 | loop fusion | bytes 10749440 | tf_op jit(solution)/shard_map/slice | solution.py:46
  126.5 2.0 slice_bitcast_fusion.12
  147.1 2.0 fusion.78
  149.1 31.3 %fusion.17 = f32[8,16,32,128]{3,0,2,1:T(8,128)} fusion(f32[8,18,32,128]{3,0,2,1:T(8,128)} %copy-done.4, f32[8,18,1,128]{3,0,2,1:T(8,128)S(1)} %collective-permute-done.8, f32[8,18,1,128]{3,0,2,1:T(8,128)S(1)} %collective-permute-done.9, f32[8,18,34,129]{3,0,2,1:T(8,128)} %get-tuple-element.70, f32[8,18,34,129]{3,0,2,1:T(8,128)} %get-tuple-element.69, ...), kind=kLoop, calls=%fused_computation.36 | loop fusion | flops 31981568 | bytes 51789824 | tf_op jit(solution)/shard_map/sub | solution.py:66
  180.5 6.7 %fusion.100 = f32[8,8,1,1]{1,0,3,2:T(8,128)S(1)} fusion(f32[8,16,32,128]{3,0,2,1:T(8,128)} %fusion.17, f32[8,16,32,128]{3,2,1,0:T(8,128)S(1)} %copy-done), kind=kOutput, calls=%fused_computation.227 | convolution fusion | flops 50331648 | bytes 4194560 | tf_op jit(solution)/shard_map/dot_general | solution.py:73
  187.2 4.7 %convolution_bitcast_fusion.4 = f32[8,8]{1,0:T(8,128)S(1)} fusion(f32[8,16,32,128]{3,0,2,1:T(8,128)S(1)} %copy-done.2), kind=kOutput, calls=%fused_computation.142 | convolution fusion | flops 50331648 | bytes 2097408 | tf_op jit(solution)/shard_map/dot_general | solution.py:73
  191.9 11.6 %all-reduce.5 = (f32[8,8]{0,1:T(8,128)S(1)}, f32[8,8]{0,1:T(8,128)S(1)}, f32[8,8]{1,0:T(8,128)S(1)}, f32[8,8]{1,0:T(8,128)S(1)}) all-reduce(f32[8,8]{0,1:T(8,128)S(1)} %copy-done.26, f32[8,8]{0,1:T(8,128)S(1)} %bitcast.147, f32[8,8]{1,0:T(8,128)S(1)} %bitcast.148, ...), channel_id=1, replica_groups=mesh['gx'=4,'gy_0'=4,'gy_1'=2,'gz'=4] {'gx'}, use_global_device_ids=true, to_apply=%region_7.9 | all-reduce | flops 256 | bytes 2048 | tf_op jit(solution)/shard_map/psum | solution.py:19
  203.5 11.9 %all-reduce.3 = (f32[8,8]{0,1:T(8,128)S(1)}, f32[8,8]{0,1:T(8,128)S(1)}, f32[8,8]{1,0:T(8,128)S(1)}, f32[8,8]{1,0:T(8,128)S(1)}) all-reduce(f32[8,8]{0,1:T(8,128)S(1)} %get-tuple-element.26, f32[8,8]{0,1:T(8,128)S(1)} %get-tuple-element.27, ...), channel_id=1, replica_groups=mesh['gx'=4,'gy_0'=4,'gy_1'=2,'gz'=4] {'gy_0'}, use_global_device_ids=true, to_apply=%region_8.10 | all-reduce | flops 256 | bytes 2048 | tf_op jit(solution)/shard_map/psum | solution.py:19
  215.3 12.6 %all-reduce.7 = (f32[8,8]{0,1:T(8,128)S(1)}, f32[8,8]{0,1:T(8,128)S(1)}, f32[8,8]{1,0:T(8,128)S(1)}, f32[8,8]{1,0:T(8,128)S(1)}) all-reduce(f32[8,8]{0,1:T(8,128)S(1)} %get-tuple-element.20, f32[8,8]{0,1:T(8,128)S(1)} %get-tuple-element.21, ...), channel_id=1, replica_groups=mesh['gx'=4,'gy_0'=4,'gy_1'=2,'gz'=4] {'gy_1'}, use_global_device_ids=true, to_apply=%region_9.11 | all-reduce | flops 256 | bytes 2048 | tf_op jit(solution)/shard_map/psum | solution.py:19
  227.9 13.8 %all-reduce.1 = (f32[8,8]{0,1:T(8,128)S(1)}, f32[8,8]{0,1:T(8,128)S(1)}, f32[8,8]{1,0:T(8,128)S(1)}, f32[8,8]{1,0:T(8,128)S(1)}) all-reduce(f32[8,8]{0,1:T(8,128)S(1)} %get-tuple-element.32, f32[8,8]{0,1:T(8,128)S(1)} %get-tuple-element.33, ...), channel_id=1, replica_groups=mesh['gx'=4,'gy_0'=4,'gy_1'=2,'gz'=4] {'gz'}, use_global_device_ids=true, to_apply=%region_10.12 | all-reduce | flops 256 | bytes 2048 | tf_op jit(solution)/shard_map/psum | solution.py:19
  247.6 4.7 %convolution_subtract_fusion.1 = f32[8,16,32,128]{3,0,2,1:T(8,128)S(1)} fusion(f32[8,16,32,128]{3,0,2,1:T(8,128)} %fusion.17, f32[8,8]{1,0:T(8,128)S(1)} %fusion.90, f32[8,16,32,128]{3,2,1,0:T(8,128)S(1)} %copy-done), kind=kOutput, calls=%fused_computation.136 | convolution fusion | flops 50855936 | bytes 6291712 | tf_op jit(solution)/shard_map/ij,ixyz->jxyz/dot_general | solution.py:83
  253.5 3.0 convolution_add_fusion.1
  256.5 1.3 collective-permute-start.12
  259.1 4.2 %fusion.95 = f32[8,16,32,128]{3,0,2,1:T(8,128)} fusion(f32[8,8]{1,0:T(8,128)S(1)} %fusion.90, f32[8,16,32,128]{3,2,1,0:T(8,128)S(1)} %copy-done.1), kind=kOutput, calls=%fused_computation.213 | convolution fusion | flops 50331648 | bytes 4194560 | tf_op jit(solution)/shard_map/ij,ixyz->jxyz/dot_general | solution.py:83
  263.5 5.3 %collective-permute-start.14 = (f32[8,18,1,128]{3,0,2,1:T(8,128)S(1)}, f32[8,18,1,128]{3,0,2,1:T(8,128)S(1)}, u32[]{:S(2)}, u32[]{:S(2)}) collective-permute-start(f32[8,18,1,128]{3,0,2,1:T(8,128)S(1)} %get-tuple-element.75), channel_id=1, source_target_pairs={{0,4},{4,8},{8,12},{12,16},{16,20},{20,24},{24,28},{1,5},{5,9},{9,... | collective-permute-start | bytes 221192 | tf_op jit(solution)/shard_map/ppermute | solution.py:31
  268.9 3.6 collective-permute-start.15
  272.4 5.3 %convolution_bitcast_fusion.1 = f32[8,8]{1,0:T(8,128)} fusion(f32[8,16,32,128]{3,0,2,1:T(8,128)S(1)} %convolution_subtract_fusion.1), kind=kOutput, calls=%fused_computation.138 | convolution fusion | flops 50331648 | bytes 2097408 | tf_op jit(solution)/shard_map/dot_general | solution.py:73
  277.9 3.0 fusion.106
  280.9 3.4 copy.215
  285.7 3.4 copy.217
  289.1 4.6 %collective-permute-start.17 = (f32[8,18,34,1]{2,0,3,1:T(8,128)}, f32[8,18,34,1]{2,0,3,1:T(8,128)}, u32[]{:S(2)}, u32[]{:S(2)}) collective-permute-start(f32[8,18,34,1]{2,0,3,1:T(8,128)} %copy.217), channel_id=1, source_target_pairs={{0,1},{1,2},{2,3},{4,5},{5,6},{6,7},{8,9},{9,10},{10,11},{12,13},{... | collective-permute-start | bytes 58760 | tf_op jit(solution)/shard_map/ppermute | solution.py:31
  293.7 2.5 pad_maximum_fusion.6
  296.2 3.5 copy.216
  299.6 3.4 copy.218
  303.1 7.9 %pad_maximum_fusion.3 = (f32[8,18,34,129]{3,0,2,1:T(8,128)}, f32[8,18,34,129]{3,0,2,1:T(8,128)}) fusion(f32[8,18,34,1]{3,0,2,1:T(8,128)} %copy.216, f32[8,18,1,128]{3,0,2,1:T(8,128)S(1)} %collective-permute-done.15, f32[8,1,32,128]{3,0,2,1:T(8,128)S(1)} %collective-permute-done.13, f32[8,16,32,128]{3,0,2,1:T(8,128)S(1)} %convolution_add_fusion.1, ...), kind=kLoop, calls=%fused_computation.4 | loop fusion | flops 6315840 | bytes 7598592 | tf_op jit(solution)/shard_map/concatenate | solution.py:29
  311.0 29.6 %fusion.30 = f32[8,16,32,128]{3,0,2,1:T(8,128)} fusion(f32[8,18,34,129]{3,0,2,1:T(8,128)} %get-tuple-element.66, f32[8,18,34,129]{3,0,2,1:T(8,128)} %get-tuple-element.65, f32[8,18,33,128]{3,0,2,1:T(8,128)} %get-tuple-element.74, f32[8,18,33,128]{3,0,2,1:T(8,128)} %get-tuple-element.73, f32[8,16,32,128]{3,0,2,1:T(8,128)S(1)} %convolution_add_fusion.1, ...), kind=kLoop, calls=%fused_computation.50 | loop fusion | flops 28835840 | bytes 61865984 | tf_op jit(solution)/shard_map/sub | solution.py:66
  340.6 6.2 %convolution_bitcast_fusion.2 = f32[8,8]{0,1:T(8,128)S(1)} fusion(f32[8,16,32,128]{3,0,2,1:T(8,128)S(1)} %convolution_add_fusion.1, f32[8,16,32,128]{3,0,2,1:T(8,128)} %fusion.30), kind=kOutput, calls=%fused_computation.139 | convolution fusion | flops 50331648 | bytes 4194560 | tf_op jit(solution)/shard_map/dot_general | solution.py:73
  346.8 7.7 %all-reduce.4 = (f32[8,8]{1,0:T(8,128)S(1)}, f32[8,8]{0,1:T(8,128)S(1)}) all-reduce(f32[8,8]{1,0:T(8,128)S(1)} %copy-done.25, f32[8,8]{0,1:T(8,128)S(1)} %convolution_bitcast_fusion.2), channel_id=1, replica_groups=mesh['gx'=4,'gy_0'=4,'gy_1'=2,'gz'=4] {'gx'}, use_global_device_ids=true, to_apply=%region_23.0 | all-reduce | flops 128 | bytes 1024 | tf_op jit(solution)/shard_map/psum | solution.py:19
  354.4 6.9 %all-reduce.2 = (f32[8,8]{1,0:T(8,128)S(1)}, f32[8,8]{0,1:T(8,128)S(1)}) all-reduce(f32[8,8]{1,0:T(8,128)S(1)} %get-tuple-element.24, f32[8,8]{0,1:T(8,128)S(1)} %get-tuple-element.25), channel_id=1, replica_groups=mesh['gx'=4,'gy_0'=4,'gy_1'=2,'gz'=4] {'gy_0'}, use_global_device_ids=true, to_apply=%region_24.0 | all-reduce | flops 128 | bytes 1024 | tf_op jit(solution)/shard_map/psum | solution.py:19
  361.3 7.8 %all-reduce.6 = (f32[8,8]{1,0:T(8,128)S(1)}, f32[8,8]{0,1:T(8,128)S(1)}) all-reduce(f32[8,8]{1,0:T(8,128)S(1)} %get-tuple-element.18, f32[8,8]{0,1:T(8,128)S(1)} %get-tuple-element.19), channel_id=1, replica_groups=mesh['gx'=4,'gy_0'=4,'gy_1'=2,'gz'=4] {'gy_1'}, use_global_device_ids=true, to_apply=%region_25.28 | all-reduce | flops 128 | bytes 1024 | tf_op jit(solution)/shard_map/psum | solution.py:19
  369.1 6.3 %all-reduce = (f32[8,8]{1,0:T(8,128)S(1)}, f32[8,8]{0,1:T(8,128)S(1)}) all-reduce(f32[8,8]{1,0:T(8,128)S(1)} %get-tuple-element.30, f32[8,8]{0,1:T(8,128)S(1)} %get-tuple-element.31), channel_id=1, replica_groups=mesh['gx'=4,'gy_0'=4,'gy_1'=2,'gz'=4] {'gz'}, use_global_device_ids=true, to_apply=%region_26.29 | all-reduce | flops 128 | bytes 1024 | tf_op jit(solution)/shard_map/psum | solution.py:19
  378.7 4.1 %convolution_subtract_fusion = f32[8,16,32,128]{3,0,2,1:T(8,128)S(1)} fusion(f32[8,16,32,128]{3,0,2,1:T(8,128)} %copy-done.3, f32[8,8,1,1]{0,1,3,2:T(8,128)S(1)} %convolution_bitcast_fusion, f32[8,16,32,128]{3,0,2,1:T(8,128)} %fusion.30), kind=kOutput, calls=%fused_computation.133 | convolution fusion | flops 50855936 | bytes 6291712 | tf_op jit(solution)/shard_map/ij,ixyz->jxyz/dot_general | solution.py:83
  382.9 1.7 copy.225
  385.0 1.9 convolution_add_fusion
  386.9 1.7 copy.224
  (155 shorter events, 39.6 us)
Async XLA Ops:
  0.6 15.1 %copy-start = (f32[8,16,32,128]{3,2,1,0:T(8,128)S(1)}, f32[8,16,32,128]{3,2,1,0:T(8,128)}, u32[]{:S(2)}) copy-start(f32[8,16,32,128]{3,2,1,0:T(8,128)} %param.5) | copy-start | bytes 6291460
  4.0 11.0 %copy-start.7 = (f32[8,16,32,128]{3,0,2,1:T(8,128)}, f32[8,16,32,128]{3,0,2,1:T(8,128)S(1)}, u32[]{:S(2)}) copy-start(f32[8,16,32,128]{3,0,2,1:T(8,128)S(1)} %copy.170) | copy-start | bytes 6291460
  4.1 11.0 %collective-permute-start.6 = (f32[8,1,32,128]{3,0,2,1:T(8,128)S(1)}, f32[8,1,32,128]{3,0,2,1:T(8,128)S(1)}, u32[]{:S(2)}, u32[]{:S(2)}) collective-permute-start(f32[8,1,32,128]{3,0,2,1:T(8,128)S(1)} %get-tuple-element.82), channel_id=1, source_target_pairs={{0,32},{32,64},{64,96},{1,33},{33,65},{65,97},{2,34},{34,66},{66,9... | collective-permute-start | bytes 393224 | tf_op jit(solution)/shard_map/ppermute | solution.py:31
  9.2 38.9 %collective-permute-start = (f32[14,1,32,128]{3,2,1,0:T(8,128)S(1)}, f32[14,1,32,128]{3,2,1,0:T(8,128)S(1)}, u32[]{:S(2)}, u32[]{:S(2)}) collective-permute-start(f32[14,1,32,128]{3,2,1,0:T(8,128)S(1)} %get-tuple-element.64), channel_id=1, source_target_pairs={{0,32},{32,64},{64,96},{1,33},{33,65},{65,97},{2,34},{34,66},{66,9... | collective-permute-start | bytes 688136 | tf_op jit(solution)/shard_map/ppermute | solution.py:31
  12.4 38.2 %collective-permute-start.1 = (f32[14,1,32,128]{3,2,1,0:T(8,128)S(1)}, f32[14,1,32,128]{3,2,1,0:T(8,128)S(1)}, u32[]{:S(2)}, u32[]{:S(2)}) collective-permute-start(f32[14,1,32,128]{3,2,1,0:T(8,128)S(1)} %get-tuple-element.63), channel_id=1, source_target_pairs={{32,0},{64,32},{96,64},{33,1},{65,33},{97,65},{34,2},{66,34},{98,6... | collective-permute-start | bytes 688136 | tf_op jit(solution)/shard_map/ppermute | solution.py:33
  13.7 9.3 %collective-permute-start.7 = (f32[8,1,32,128]{3,0,2,1:T(8,128)S(1)}, f32[8,1,32,128]{3,0,2,1:T(8,128)S(1)}, u32[]{:S(2)}, u32[]{:S(2)}) collective-permute-start(f32[8,1,32,128]{3,0,2,1:T(8,128)S(1)} %get-tuple-element.81), channel_id=1, source_target_pairs={{32,0},{64,32},{96,64},{33,1},{65,33},{97,65},{34,2},{66,34},{98,6... | collective-permute-start | bytes 393224 | tf_op jit(solution)/shard_map/ppermute | solution.py:33
  15.0 0.7 copy-start.23
  15.7 14.4 %copy-start.6 = (f32[14,16,32,128]{3,2,1,0:T(8,128)S(1)}, f32[14,16,32,128]{3,2,1,0:T(8,128)}, u32[]{:S(2)}) copy-start(f32[14,16,32,128]{3,2,1,0:T(8,128)} %param.6) | copy-start | bytes 11010052
  23.0 8.2 %copy-start.24 = (f32[8,1,32,128]{3,0,2,1:T(8,128)}, f32[8,1,32,128]{3,0,2,1:T(8,128)S(1)}, u32[]{:S(2)}) copy-start(f32[8,1,32,128]{3,0,2,1:T(8,128)S(1)} %collective-permute-done.7) | copy-start | bytes 393220
  23.0 10.8 %copy-start.4 = (f32[8,18,32,128]{3,0,2,1:T(8,128)}, f32[8,18,32,128]{3,0,2,1:T(8,128)S(1)}, u32[]{:S(2)}) copy-start(f32[8,18,32,128]{3,0,2,1:T(8,128)S(1)} %constant_dynamic-update-slice_fusion.3) | copy-start | bytes 7077892
  23.1 8.1 %collective-permute-start.8 = (f32[8,18,1,128]{3,0,2,1:T(8,128)S(1)}, f32[8,18,1,128]{3,0,2,1:T(8,128)S(1)}, u32[]{:S(2)}, u32[]{:S(2)}) collective-permute-start(f32[8,18,1,128]{3,0,2,1:T(8,128)S(1)} %get-tuple-element.78), channel_id=1, source_target_pairs={{0,4},{4,8},{8,12},{12,16},{16,20},{20,24},{24,28},{1,5},{5,9},{9,... | collective-permute-start | bytes 221192 | tf_op jit(solution)/shard_map/ppermute | solution.py:31
  28.2 5.7 %collective-permute-start.9 = (f32[8,18,1,128]{3,0,2,1:T(8,128)S(1)}, f32[8,18,1,128]{3,0,2,1:T(8,128)S(1)}, u32[]{:S(2)}, u32[]{:S(2)}) collective-permute-start(f32[8,18,1,128]{3,0,2,1:T(8,128)S(1)} %get-tuple-element.77), channel_id=1, source_target_pairs={{4,0},{8,4},{12,8},{16,12},{20,16},{24,20},{28,24},{5,1},{9,5},{13... | collective-permute-start | bytes 221192 | tf_op jit(solution)/shard_map/ppermute | solution.py:33
  39.8 23.2 %collective-permute-start.10 = (f32[8,18,34,1]{2,0,3,1:T(8,128)S(1)}, f32[8,18,34,1]{2,0,3,1:T(8,128)S(1)}, u32[]{:S(2)}, u32[]{:S(2)}) collective-permute-start(f32[8,18,34,1]{2,0,3,1:T(8,128)S(1)} %copy.174), channel_id=1, source_target_pairs={{1,0},{2,1},{3,2},{5,4},{6,5},{7,6},{9,8},{10,9},{11,10},{13,12},{... | collective-permute-start | bytes 58760 | tf_op jit(solution)/shard_map/ppermute | solution.py:33
  43.9 21.7 %collective-permute-start.11 = (f32[8,18,34,1]{2,0,3,1:T(8,128)S(1)}, f32[8,18,34,1]{2,0,3,1:T(8,128)S(1)}, u32[]{:S(2)}, u32[]{:S(2)}) collective-permute-start(f32[8,18,34,1]{2,0,3,1:T(8,128)S(1)} %copy.176), channel_id=1, source_target_pairs={{0,1},{1,2},{2,3},{4,5},{5,6},{6,7},{8,9},{9,10},{10,11},{12,13},{... | collective-permute-start | bytes 58760 | tf_op jit(solution)/shard_map/ppermute | solution.py:31
  50.7 1.9 copy-start.5
  52.8 15.4 %collective-permute-start.2 = (f32[14,18,1,128]{3,0,2,1:T(8,128)S(1)}, f32[14,18,1,128]{3,0,2,1:T(8,128)S(1)}, u32[]{:S(2)}, u32[]{:S(2)}) collective-permute-start(f32[14,18,1,128]{3,0,2,1:T(8,128)S(1)} %copy.160), channel_id=1, source_target_pairs={{0,4},{4,8},{8,12},{12,16},{16,20},{20,24},{24,28},{1,5},{5,9},{9,... | collective-permute-start | bytes 387080 | tf_op jit(solution)/shard_map/ppermute | solution.py:31
  55.1 13.2 %collective-permute-start.3 = (f32[14,18,1,128]{3,0,2,1:T(8,128)S(1)}, f32[14,18,1,128]{3,0,2,1:T(8,128)S(1)}, u32[]{:S(2)}, u32[]{:S(2)}) collective-permute-start(f32[14,18,1,128]{3,0,2,1:T(8,128)S(1)} %copy.161), channel_id=1, source_target_pairs={{4,0},{8,4},{12,8},{16,12},{20,16},{24,20},{28,24},{5,1},{9,5},{13... | collective-permute-start | bytes 387080 | tf_op jit(solution)/shard_map/ppermute | solution.py:33
  80.8 17.3 %collective-permute-start.4 = (f32[14,18,34,1]{2,0,3,1:T(8,128)S(1)}, f32[14,18,34,1]{2,0,3,1:T(8,128)S(1)}, u32[]{:S(2)}, u32[]{:S(2)}) collective-permute-start(f32[14,18,34,1]{2,0,3,1:T(8,128)S(1)} %copy.164), channel_id=1, source_target_pairs={{0,1},{1,2},{2,3},{4,5},{5,6},{6,7},{8,9},{9,10},{10,11},{12,13},{... | collective-permute-start | bytes 102824 | tf_op jit(solution)/shard_map/ppermute | solution.py:31
  88.3 13.3 %collective-permute-start.5 = (f32[14,18,34,1]{2,0,3,1:T(8,128)S(1)}, f32[14,18,34,1]{2,0,3,1:T(8,128)S(1)}, u32[]{:S(2)}, u32[]{:S(2)}) collective-permute-start(f32[14,18,34,1]{2,0,3,1:T(8,128)S(1)} %copy.165), channel_id=1, source_target_pairs={{1,0},{2,1},{3,2},{5,4},{6,5},{7,6},{9,8},{10,9},{11,10},{13,12},{... | collective-permute-start | bytes 102824 | tf_op jit(solution)/shard_map/ppermute | solution.py:33
  126.5 2.0 copy-start.10
  126.5 2.1 copy-start.11
  128.6 2.2 copy-start.9
  135.1 2.2 copy-start.21
  135.1 3.1 copy-start.20
  135.5 3.6 copy-start.19
  135.5 4.3 %copy-start.18 = (f32[16,34,130]{2,1,0:T(8,128)S(1)}, f32[16,34,130]{2,1,0:T(8,128)}, u32[]{:S(2)}) copy-start(f32[16,34,130]{2,1,0:T(8,128)} %get-tuple-element.51) | copy-start | bytes 848644
  135.5 5.2 %copy-start.17 = (f32[16,34,130]{2,1,0:T(8,128)S(1)}, f32[16,34,130]{2,1,0:T(8,128)}, u32[]{:S(2)}) copy-start(f32[16,34,130]{2,1,0:T(8,128)} %get-tuple-element.50) | copy-start | bytes 848644
  135.6 5.9 %copy-start.16 = (f32[16,34,130]{2,1,0:T(8,128)S(1)}, f32[16,34,130]{2,1,0:T(8,128)}, u32[]{:S(2)}) copy-start(f32[16,34,130]{2,1,0:T(8,128)} %get-tuple-element.49) | copy-start | bytes 848644
  136.4 5.8 %copy-start.15 = (f32[16,34,130]{2,1,0:T(8,128)S(1)}, f32[16,34,130]{2,1,0:T(8,128)}, u32[]{:S(2)}) copy-start(f32[16,34,130]{2,1,0:T(8,128)} %get-tuple-element.48) | copy-start | bytes 848644
  136.6 6.5 %copy-start.14 = (f32[16,34,130]{2,1,0:T(8,128)S(1)}, f32[16,34,130]{2,1,0:T(8,128)}, u32[]{:S(2)}) copy-start(f32[16,34,130]{2,1,0:T(8,128)} %get-tuple-element.47) | copy-start | bytes 848644
  137.4 6.6 %copy-start.13 = (f32[16,34,130]{2,1,0:T(8,128)S(1)}, f32[16,34,130]{2,1,0:T(8,128)}, u32[]{:S(2)}) copy-start(f32[16,34,130]{2,1,0:T(8,128)} %get-tuple-element.46) | copy-start | bytes 848644
  144.7 2.4 copy-start.22
  149.1 31.3 %copy-start.12 = (f32[16,32,128]{2,1,0:T(8,128)}, f32[16,32,128]{2,1,0:T(8,128)S(1)}, u32[]{:S(2)}) copy-start(f32[16,32,128]{2,1,0:T(8,128)S(1)} %get-tuple-element.87) | copy-start | bytes 786436
  180.4 6.7 %copy-start.2 = (f32[8,16,32,128]{3,0,2,1:T(8,128)S(1)}, f32[8,16,32,128]{3,0,2,1:T(8,128)}, u32[]{:S(2)}) copy-start(f32[8,16,32,128]{3,0,2,1:T(8,128)} %fusion.17) | copy-start | bytes 6291460
  187.2 4.7 %copy-start.26 = (f32[8,8]{0,1:T(8,128)S(1)}, f32[8,8]{0,1:T(8,128)}, u32[]{:S(2)}) copy-start(f32[8,8]{0,1:T(8,128)} %convolution_bitcast_fusion.5) | copy-start | bytes 772
  247.6 5.8 %copy-start.1 = (f32[8,16,32,128]{3,2,1,0:T(8,128)S(1)}, f32[8,16,32,128]{3,2,1,0:T(8,128)}, u32[]{:S(2)}) copy-start(f32[8,16,32,128]{3,2,1,0:T(8,128)} %param.5) | copy-start | bytes 6291460
  252.4 20.1 %copy-start.3 = (f32[8,16,32,128]{3,0,2,1:T(8,128)}, f32[8,16,32,128]{3,0,2,1:T(8,128)S(1)}, u32[]{:S(2)}) copy-start(f32[8,16,32,128]{3,0,2,1:T(8,128)S(1)} %convolution_subtract_fusion.1) | copy-start | bytes 6291460
  256.5 6.8 %collective-permute-start.12 = (f32[8,1,32,128]{3,0,2,1:T(8,128)S(1)}, f32[8,1,32,128]{3,0,2,1:T(8,128)S(1)}, u32[]{:S(2)}, u32[]{:S(2)}) collective-permute-start(f32[8,1,32,128]{3,0,2,1:T(8,128)S(1)} %get-tuple-element.79), channel_id=1, source_target_pairs={{0,32},{32,64},{64,96},{1,33},{33,65},{65,97},{2,34},{34,66},{66,9... | collective-permute-start | bytes 393224 | tf_op jit(solution)/shard_map/ppermute | solution.py:31
  257.8 5.7 %collective-permute-start.13 = (f32[8,1,32,128]{3,0,2,1:T(8,128)S(1)}, f32[8,1,32,128]{3,0,2,1:T(8,128)S(1)}, u32[]{:S(2)}, u32[]{:S(2)}) collective-permute-start(f32[8,1,32,128]{3,0,2,1:T(8,128)S(1)} %get-tuple-element.80), channel_id=1, source_target_pairs={{32,0},{64,32},{96,64},{33,1},{65,33},{97,65},{34,2},{66,34},{98,6... | collective-permute-start | bytes 393224 | tf_op jit(solution)/shard_map/ppermute | solution.py:33
  263.5 14.2 %collective-permute-start.14 = (f32[8,18,1,128]{3,0,2,1:T(8,128)S(1)}, f32[8,18,1,128]{3,0,2,1:T(8,128)S(1)}, u32[]{:S(2)}, u32[]{:S(2)}) collective-permute-start(f32[8,18,1,128]{3,0,2,1:T(8,128)S(1)} %get-tuple-element.75), channel_id=1, source_target_pairs={{0,4},{4,8},{8,12},{12,16},{16,20},{20,24},{24,28},{1,5},{5,9},{9,... | collective-permute-start | bytes 221192 | tf_op jit(solution)/shard_map/ppermute | solution.py:31
  268.9 8.9 %collective-permute-start.15 = (f32[8,18,1,128]{3,0,2,1:T(8,128)S(1)}, f32[8,18,1,128]{3,0,2,1:T(8,128)S(1)}, u32[]{:S(2)}, u32[]{:S(2)}) collective-permute-start(f32[8,18,1,128]{3,0,2,1:T(8,128)S(1)} %get-tuple-element.76), channel_id=1, source_target_pairs={{4,0},{8,4},{12,8},{16,12},{20,16},{24,20},{28,24},{5,1},{9,5},{13... | collective-permute-start | bytes 221192 | tf_op jit(solution)/shard_map/ppermute | solution.py:33
  284.4 11.8 %collective-permute-start.16 = (f32[8,18,34,1]{2,0,3,1:T(8,128)}, f32[8,18,34,1]{2,0,3,1:T(8,128)}, u32[]{:S(2)}, u32[]{:S(2)}) collective-permute-start(f32[8,18,34,1]{2,0,3,1:T(8,128)} %copy.215), channel_id=1, source_target_pairs={{1,0},{2,1},{3,2},{5,4},{6,5},{7,6},{9,8},{10,9},{11,10},{13,12},{... | collective-permute-start | bytes 58760 | tf_op jit(solution)/shard_map/ppermute | solution.py:33
  289.1 10.5 %collective-permute-start.17 = (f32[8,18,34,1]{2,0,3,1:T(8,128)}, f32[8,18,34,1]{2,0,3,1:T(8,128)}, u32[]{:S(2)}, u32[]{:S(2)}) collective-permute-start(f32[8,18,34,1]{2,0,3,1:T(8,128)} %copy.217), channel_id=1, source_target_pairs={{0,1},{1,2},{2,3},{4,5},{5,6},{6,7},{8,9},{9,10},{10,11},{12,13},{... | collective-permute-start | bytes 58760 | tf_op jit(solution)/shard_map/ppermute | solution.py:31
  340.5 6.2 %copy-start.25 = (f32[8,8]{1,0:T(8,128)S(1)}, f32[8,8]{1,0:T(8,128)}, u32[]{:S(2)}) copy-start(f32[8,8]{1,0:T(8,128)} %convolution_bitcast_fusion.1) | copy-start | bytes 772
  382.8 2.2 copy-start.8
where the time goes:
time: 396 us; the launch traced here: 389 us
  other arithmetic  107 us (27%)
  local copies, waits for them, and re-layouts  95.3 us (24%)
  blocking collectives  78.6 us (20%)
  starting transfers between devices  49.6 us (13%)
  matrix products  48.1 us (12%)
  waiting for transfers between devices  8.57 us (2%)
    psum x8, blocking collectives, over_axes(): x = lax.psum(x, axis)  78.6 us
    sub x2, other arithmetic, operate(): result = result - behind_w[None] * window(field, fmargin, depth, back)  60.9 us
    concatenate x7, other arithmetic, with_halo(): jnp.concatenate([lax.ppermute(tail, axis, [(i, (i + 1) % count) for i in...  34.9 us
    ppermute x9, starting transfers between devices, with_halo(): lax.ppermute(tail, axis, [(i, (i + 1) % count) for i in range(ends)])  33.5 us
    dot_general x5, matrix products, gram(): lax.dot_general(flat_l, flat_r, (((1,), (1,)), ((), ())), precision=lax.P...  28.4 us
    slice x35, local copies, waits for them, and re-layouts, window(): lax.slice_in_dim(result, begin, begin + inner + 2 * depth, axis=dim)  28.2 us
    dot_general x5, matrix products, combine(): jnp.einsum('ij,ixyz->jxyz', coef, field, precision=lax.Precision.HIGHEST)  17.8 us
    slice x9, local copies, waits for them, and re-layouts, with_halo(): head = lax.slice_in_dim(cells, 0, width, axis=dim)  17.3 us
  transfers between devices with their start and end apart: 18, of which 3 were waited for; matrix products, arithmetic and copies ran while one was open for 16% of the time, Pallas kernels for 0%

commit v1 on v0

v1 whole, which is shorter than its diff:
```python
import functools

import jax
import jax.numpy as jnp
from jax import lax
from jax.experimental import pallas as pl
from jax.experimental.pallas import tpu as pltpu
from jax.sharding import PartitionSpec as P

F32 = jnp.float32
N = 8
FORWARD = [
    (a, b, c) for a in (-1, 0, 1) for b in (-1, 0, 1) for c in (-1, 0, 1) if (a, b, c) > (0, 0, 0)
]
INDEX = {o: k + 1 for k, o in enumerate(FORWARD)}
PLANE = [(a, b) for a in (-1, 0, 1) for b in (-1, 0, 1)]
SLOTS = [(0, 0), (0, 1), (1, -1), (1, 0), (1, 1)]
LOW = [INDEX[(a, b, 1)] for a, b in SLOTS]
UP = [INDEX[(a, b, -1)] if (a, b) != (0, 0) else INDEX[(0, 0, 1)] for a, b in SLOTS]
DIRS = [
    (a, b, c) for a in (-1, 0, 1) for b in (-1, 0, 1) for c in (-1, 0, 1) if (a, b, c) != (0, 0, 0)
]
WRANGE = {(1, 0): (5, 9), (1, 1): (11, 3), (1, -1): (5, 3), (0, 1): (2, 12), (0, -1): (5, 3)}
WDIRS = list(WRANGE)
PAIRS = [(i, j) for i in range(N) for j in range(i, N)]
TOP = 8


def lanes():
    return lax.broadcasted_iota(jnp.int32, (8, 128), 1)


def rows():
    return lax.broadcasted_iota(jnp.int32, (8, 128), 0)


def splat_row(m, k):
    return jnp.broadcast_to(m[k : k + 1, :], (8, 128))


def splat_col(m, k):
    return jnp.broadcast_to(m[:, k : k + 1], (8, 128))


def row_sum(m):
    return jnp.broadcast_to(jnp.sum(m, axis=1, keepdims=True), (8, 128))


def shift(m, amount):
    amount = amount % 128
    return pltpu.roll(m, amount, 1) if amount else m


def product(a, b):
    total = splat_col(a, 0) * splat_row(b, 0)
    for k in range(1, N):
        total = total + splat_col(a, k) * splat_row(b, k)
    return total


def product_t(a, b):
    same = lanes() == rows()
    total = None
    for k in range(N):
        column = row_sum(jnp.where(same, splat_row(a, k), 0.0))
        term = column * splat_row(b, k)
        total = term if total is None else total + term
    return total


def eliminate(m):
    row_id = rows()
    for k in range(N):
        pivot = splat_row(m, k)
        scaled = pivot / splat_col(pivot, k)
        m = jnp.where(row_id == k, scaled, m - splat_col(m, k) * scaled)
    return m


def pack_lanes(parts):
    lane = lanes()
    total = None
    for slot, part in enumerate(parts):
        here = (lane >= 8 * slot) & (lane < 8 * slot + 8)
        term = jnp.where(here, shift(part, 8 * slot), 0.0)
        total = term if total is None else total + term
    return total


def kernel(
    sizes,
    x_ref,
    w_ref,
    q_out,
    s_out,
    c_out,
    V,
    Q,
    W,
    WW,
    WE,
    R,
    PP,
    LPP,
    PQ,
    LPQ,
    G,
    GW,
    S,
    ARS,
    ARL,
    load_sem,
    out_sem,
    send1,
    recv1,
    send2,
    recv2,
    ar_send,
    ar_recv,
):
    names = ("gx", "gy", "gz")
    nx, ny, nz = sizes
    me = tuple(lax.axis_index(n) for n in names)

    def exists(d):
        cond = None
        for pos, step, count in zip(me, d, sizes):
            term = None
            if step > 0:
                term = pos < count - 1
            elif step < 0:
                term = pos > 0
            if term is not None:
                cond = term if cond is None else cond & term
        return cond

    def opposite(d):
        return tuple(-t for t in d)

    def target(d):
        return tuple(pos + step for pos, step in zip(me, d))

    def peer(axis, p):
        return tuple(
            lax.rem(pos + p, sizes[i]) if i == axis else pos for i, pos in enumerate(me)
        )

    load_x = pltpu.make_async_copy(x_ref, V.at[:, pl.ds(1, 16), pl.ds(TOP, 32)], load_sem.at[0])
    load_w = pltpu.make_async_copy(w_ref, W.at[:, pl.ds(1, 16), pl.ds(TOP, 32)], load_sem.at[1])
    load_x.start()
    load_w.start()

    zero = jnp.zeros((8, 128), F32)

    def clear_padded(buf, first, last):
        for field in range(buf.shape[0]):
            for plane in (first, last):
                if plane is not None:
                    for t in range(6):
                        buf[field, plane, pl.ds(8 * t, 8)] = zero

        def body(p, carry):
            for field in range(buf.shape[0]):
                buf[field, p, pl.ds(0, 8)] = zero
                buf[field, p, pl.ds(40, 8)] = zero
            return carry

        lax.fori_loop(1, 17, body, 0)

    clear_padded(V, 0, 17)
    clear_padded(Q, 0, 17)
    clear_padded(W, 0, None)

    def clear_landing(i, carry):
        for t in range(6):
            for s in range(2):
                for k in range(2):
                    LPP[s, k, i, pl.ds(8 * t, 8)] = zero
                LPQ[s, i, pl.ds(8 * t, 8)] = zero
        return carry

    lax.fori_loop(0, 4, clear_landing, 0)

    barrier = pltpu.get_barrier_semaphore()
    for d in DIRS:

        @pl.when(exists(d))
        def _():
            pl.semaphore_signal(
                barrier, inc=1, device_id=target(d), device_id_type=pl.DeviceIdType.MESH
            )

    for axis in range(3):
        for p in range(1, sizes[axis]):
            pl.semaphore_signal(
                barrier, inc=1, device_id=peer(axis, p), device_id_type=pl.DeviceIdType.MESH
            )
    span = []
    for pos, count in zip(me, sizes):
        span.append(1 + (pos > 0).astype(jnp.int32) + (pos < count - 1).astype(jnp.int32))
    pl.semaphore_wait(
        barrier, span[0] * span[1] * span[2] - 1 + (nx - 1) + (ny - 1) + (nz - 1)
    )

    def along(step, whole, plus, minus):
        if step == 0:
            return (pl.ds(*whole), pl.ds(*whole))
        src, dst = plus if step > 0 else minus
        return (pl.ds(src, 1), pl.ds(dst, 1))

    def field_part(d, buf, sends, recvs):
        i = DIRS.index(d)
        xs, xd = along(d[0], (1, 16), (16, 0), (1, 17))
        ys, yd = along(d[1], (TOP, 32), (TOP + 31, TOP - 1), (TOP, TOP + 32))
        return pltpu.make_async_remote_copy(
            src_ref=buf.at[:, xs, ys],
            dst_ref=buf.at[:, xd, yd],
            send_sem=sends.at[i],
            recv_sem=recvs.at[i],
            device_id=target(d),
            device_id_type=pl.DeviceIdType.MESH,
        )

    def weight_part(d):
        i = 26 + WDIRS.index((d[0], d[1]))
        k0, kn = WRANGE[(d[0], d[1])]
        xs, xd = along(d[0], (1, 16), (16, 0), (1, 17))
        ys, yd = along(d[1], (TOP, 32), (TOP + 31, TOP - 1), (TOP, TOP + 32))
        return pltpu.make_async_remote_copy(
            src_ref=W.at[pl.ds(k0, kn), xs, ys],
            dst_ref=W.at[pl.ds(k0, kn), xd, yd],
            send_sem=send1.at[i],
            recv_sem=recv1.at[i],
            device_id=target(d),
            device_id_type=pl.DeviceIdType.MESH,
        )

    def column_part(d, both):
        i = DIRS.index(d)
        side = 0 if d[2] > 0 else 1
        if d[0] == 0:
            gs, gd = pl.ds(0, 2), pl.ds(1, 2)
        elif d[0] > 0:
            gs, gd = pl.ds(1, 1), pl.ds(0, 1)
        else:
            gs, gd = pl.ds(0, 1), pl.ds(3, 1)
        if d[1] == 0:
            ys, yd = pl.ds(0, 32), pl.ds(TOP, 32)
        elif d[1] > 0:
            ys, yd = pl.ds(31, 1), pl.ds(TOP - 1, 1)
        else:
            ys, yd = pl.ds(0, 1), pl.ds(TOP + 32, 1)
        src = PP.at[:, gs, ys] if both else PQ.at[gs, ys]
        dst = LPP.at[side, :, gd, yd] if both else LPQ.at[side, gd, yd]
        return pltpu.make_async_remote_copy(
            src_ref=src,
            dst_ref=dst,
            send_sem=(send1 if both else send2).at[i],
            recv_sem=(recv1 if both else recv2).at[i],
            device_id=target(d),
            device_id_type=pl.DeviceIdType.MESH,
        )

    def start_if(d, copy):
        @pl.when(exists(d))
        def _():
            copy.start()

    def recv_if(d, copy):
        @pl.when(exists(opposite(d)))
        def _():
            copy.wait_recv()

    def sent_if(d, copy):
        @pl.when(exists(d))
        def _():
            copy.wait_send()

    flat = sorted((d for d in DIRS if d[2] == 0), key=lambda d: abs(d[1]))
    flat_w = [(a, b, 0) for a, b in WDIRS]
    cols = [d for d in DIRS if d[2] != 0]

    lane = lanes()
    odd = lax.rem(lane, 2) == 1
    first = lane == 0
    last = lane == 127
    half = lane // 2

    def pack_fields(buf, dst):
        def body(i, carry):
            xg = i // 4
            yt = lax.rem(i, 4)
            r0 = pl.multiple_of(8 * yt, 8)
            total = zero
            for xm in range(8):
                for f in range(N):
                    v = buf[f, xg * 8 + xm + 1, pl.ds(r0 + TOP, 8)]
                    total = jnp.where(
                        half == 8 * xm + f, shift(v, 16 * xm + 2 * f + 1), total
                    )
            dst(xg, r0, total)
            return carry

        lax.fori_loop(0, 8, body, 0)

    def pack_weights():
        def body(i, carry):
            xg = i // 4
            yt = lax.rem(i, 4)
            r0 = pl.multiple_of(8 * yt, 8)
            total = zero
            for xm in range(8):
                for j in range(5):
                    lo = W[LOW[j], xg * 8 + xm + 1, pl.ds(r0 + TOP, 8)]
                    up = W[UP[j], xg * 8 + xm + 1, pl.ds(r0 + TOP, 8)]
                    v = jnp.where(first, up, lo)
                    total = jnp.where(
                        half == 8 * xm + j, shift(v, 16 * xm + 2 * j + 1), total
                    )
            PP[1, xg, pl.ds(r0, 8)] = total
            return carry

        lax.fori_loop(0, 8, body, 0)

    def unpack(get, dst, planes):
        def body(t, carry):
            r0 = pl.multiple_of(8 * t, 8)
            merged = {}
            for xi in range(planes):
                if xi == 0:
                    g, off = 0, 112
                elif xi == 17:
                    g, off = 3, 0
                else:
                    g, off = 1 + (xi - 1) // 8, 16 * ((xi - 1) % 8)
                if g not in merged:
                    merged[g] = jnp.where(odd, get(1, g, r0), get(0, g, r0))
                dst[xi, pl.ds(r0, 8)] = shift(merged[g], -off)
            return carry

        lax.fori_loop(0, 6, body, 0)

    load_x.wait()
    for d in flat:
        start_if(d, field_part(d, V, send1, recv1))

    def put_pp(xg, r0, total):
        PP[0, xg, pl.ds(r0, 8)] = total

    pack_fields(V, put_pp)
    load_w.wait()
    for d in flat_w:
        start_if(d, weight_part(d))
    pack_weights()
    for d in cols:
        start_if(d, column_part(d, True))

    def gram_loop(get):
        def body(x, acc):
            acc = list(acc)
            for t in range(4):
                left, right = get(x, t)
                for n, (i, j) in enumerate(PAIRS):
                    acc[n] = acc[n] + left[i] * right[j]
            return tuple(acc)

        return lax.fori_loop(0, 16, body, tuple(zero for _ in PAIRS))

    def spread(parts, acc, offset):
        for n, (i, j) in enumerate(PAIRS):
            total = row_sum(acc[n])
            parts[i] = jnp.where(lane == offset + j, total, parts[i])
            if i != j:
                parts[j] = jnp.where(lane == offset + i, total, parts[j])
        return parts

    def fold(parts):
        result = zero
        for i in range(N):
            total = jnp.broadcast_to(jnp.sum(parts[i], axis=0, keepdims=True), (8, 128))
            result = jnp.where(rows() == i, total, result)
        return result

    def tile(buf, x, t):
        return [buf[f, x + 1, pl.ds(TOP + 8 * t, 8)] for f in range(N)]

    def get_rr(x, t):
        v = tile(V, x, t)
        return v, v

    parts1 = spread([zero] * N, gram_loop(get_rr), 0)

    for d in flat:
        recv_if(d, field_part(d, V, send1, recv1))
    for d in flat_w:
        recv_if(d, weight_part(d))
    for d in cols:
        recv_if(d, column_part(d, True))

    unpack(lambda s, g, r0: LPP[s, 0, g, pl.ds(r0, 8)], G, 18)
    unpack(lambda s, g, r0: LPP[s, 1, g, pl.ds(r0, 8)], GW, 17)

    def m_of(a, b):
        return 3 * (a + 1) + (b + 1)

    def prepare(x, carry):
        for t in range(4):
            r0 = TOP + 8 * t

            def w_at(k, a=0, b=0):
                return W[k, x + 1 + a, pl.ds(r0 + b, 8)]

            out = pl.ds(8 * t, 8)
            own = [w_at(k) for k in range(14)]
            diag = own[0]
            for k in range(1, 14):
                diag = diag + own[k]
            ahead = zero
            behind = zero
            edge = zero
            for j, (a, b) in enumerate(SLOTS):
                halo_w = GW[x + 1 - a, pl.ds(r0 - b, 8)]
                if (a, b) == (0, 0):
                    lo_here = splat_col(halo_w, 0)
                    WE[m_of(0, 0), x, out] = -jnp.where(odd, splat_col(own[1], 127), lo_here)
                    edge = edge + jnp.where(odd, 0.0, lo_here)
                else:
                    kf = INDEX[(a, b, 0)]
                    WE[m_of(a, b), x, out] = -jnp.where(
                        odd, splat_col(own[LOW[j]], 127), splat_col(own[UP[j]], 0)
                    )
                    back = jnp.where(
                        odd, splat_col(halo_w, 2 * j + 1), splat_col(halo_w, 2 * j)
                    )
                    WE[m_of(-a, -b), x, out] = -back
                    edge = edge + back
                    WW[m_of(a, b), x, out] = -own[kf]
                    flat_back = w_at(kf, -a, -b)
                    diag = diag + flat_back
                    WW[m_of(-a, -b), x, out] = -flat_back
                    up_back = w_at(UP[j], -a, -b)
                    ahead = ahead + up_back
                    WW[9 + m_of(-a, -b), x, out] = -up_back
                    WW[18 + m_of(a, b), x, out] = -shift(own[UP[j]], 127)
                WW[9 + m_of(a, b), x, out] = -shift(own[LOW[j]], 1)
                lo_back = w_at(LOW[j], -a, -b)
                behind = behind + lo_back
                WW[18 + m_of(-a, -b), x, out] = -lo_back
            diag = diag + jnp.where(last, edge, shift(ahead, 127))
            diag = diag + jnp.where(first, edge, shift(behind, 1))
            WW[m_of(0, 0), x, out] = diag
        return carry

    lax.fori_loop(0, 16, prepare, 0)

    def edges():
        def body(x, carry):
            for t in range(4):
                total = zero
                for a, b in PLANE:
                    total = total + WE[m_of(a, b), x, pl.ds(8 * t, 8)] * G[
                        x + 1 + a, pl.ds(TOP + 8 * t + b, 8)
                    ]
                R[x, pl.ds(8 * t, 8)] = total
            return carry

        lax.fori_loop(0, 16, body, 0)

    def operate(src, put):
        def body(x, carry):
            for t in range(4):
                at = pl.ds(8 * t, 8)
                weights = [WW[m, x, at] for m in range(27)]
                halo = R[x, at]
                for f in range(N):
                    sums = [None, None, None]
                    for m, (a, b) in enumerate(PLANE):
                        v = src[f, x + 1 + a, pl.ds(TOP + 8 * t + b, 8)]
                        for c in range(3):
                            term = weights[9 * c + m] * v
                            sums[c] = term if sums[c] is None else sums[c] + term
                    side = shift(halo, -(2 * f + 1))
                    total = sums[0] + shift(jnp.where(first, side, sums[1]), 127)
                    total = total + shift(jnp.where(last, side, sums[2]), 1)
                    put(f, x, t, total)
            return carry

        lax.fori_loop(0, 16, body, 0)

    def put_q(f, x, t, value):
        Q[f, x + 1, pl.ds(TOP + 8 * t, 8)] = value

    def put_s(f, x, t, value):
        S[f, x, pl.ds(8 * t, 8)] = value

    edges()
    operate(V, put_q)

    for d in flat:
        start_if(d, field_part(d, Q, send2, recv2))

    def put_pq(xg, r0, total):
        PQ[xg, pl.ds(r0, 8)] = total

    pack_fields(Q, put_pq)
    for d in cols:
        start_if(d, column_part(d, False))
    store_q = pltpu.make_async_copy(Q.at[:, pl.ds(1, 16), pl.ds(TOP, 32)], q_out, out_sem.at[0])
    store_q.start()

    axes = (1, 0, 2)
    base = {1: 0, 0: ny, 2: ny + nx}

    def reduce_copies(which, axis):
        copies = []
        for p in range(1, sizes[axis]):
            i = base[axis] + p
            copies.append(
                pltpu.make_async_remote_copy(
                    src_ref=ARS.at[which, axis],
                    dst_ref=ARL.at[which, base[axis] + me[axis]],
                    send_sem=ar_send.at[which, i],
                    recv_sem=ar_recv.at[which, i],
                    device_id=peer(axis, p),
                    device_id_type=pl.DeviceIdType.MESH,
                )
            )
        return copies

    def reduce_start(which, axis, value):
        ARS[which, axis] = value
        ARL[which, base[axis] + me[axis]] = value
        for copy in reduce_copies(which, axis):
            copy.start()

    def reduce_finish(which, axis):
        for copy in reduce_copies(which, axis):
            copy.wait_recv()
        total = ARL[which, base[axis]]
        for i in range(1, sizes[axis]):
            total = total + ARL[which, base[axis] + i]
        return total

    def trace_body(x, acc):
        acc = list(acc)
        for t in range(4):
            r, q = tile(V, x, t), tile(Q, x, t)
            for f in range(N):
                acc[f % 4] = acc[f % 4] + r[f] * q[f]
        return tuple(acc)

    tr = lax.fori_loop(0, 16, trace_body, (zero,) * 4)
    traced = row_sum((tr[0] + tr[1]) + (tr[2] + tr[3]))
    parts1[0] = jnp.where(lane == 8, traced, parts1[0])
    reduce_start(0, axes[0], fold(parts1))

    for d in flat:
        recv_if(d, field_part(d, Q, send2, recv2))
    reduce_start(0, axes[1], reduce_finish(0, axes[0]))
    for d in cols:
        recv_if(d, column_part(d, False))

    unpack(lambda s, g, r0: LPQ[s, g, pl.ds(r0, 8)], G, 18)
    edges()
    reduce_start(0, axes[2], reduce_finish(0, axes[1]))
    operate(Q, put_s)
    store_s = pltpu.make_async_copy(S, s_out, out_sem.at[1])
    store_s.start()
    sum1 = reduce_finish(0, axes[2])

    own_gram = jnp.where(lane < 8, sum1, 0.0)
    norm = jnp.sum(row_sum(jnp.where(lane == rows(), own_gram, 0.0)), axis=0, keepdims=True)
    theta = jnp.broadcast_to(splat_row(splat_col(sum1, 8), 0), (8, 128)) / jnp.broadcast_to(
        norm, (8, 128)
    )

    def get_h1(x, t):
        r, q = tile(V, x, t), tile(Q, x, t)
        return r, [q[f] - theta * r[f] for f in range(N)]

    def get_h2(x, t):
        r, q = tile(V, x, t), tile(Q, x, t)
        z = [q[f] - theta * r[f] for f in range(N)]
        return z, z

    def get_h3(x, t):
        r, q = tile(V, x, t), tile(Q, x, t)
        s = [S[f, x, pl.ds(8 * t, 8)] for f in range(N)]
        z = [q[f] - theta * r[f] for f in range(N)]
        return z, [s[f] - theta * q[f] for f in range(N)]

    parts2 = [zero] * N
    parts2 = spread(parts2, gram_loop(get_h1), 0)
    parts2 = spread(parts2, gram_loop(get_h2), 8)
    parts2 = spread(parts2, gram_loop(get_h3), 16)
    value = fold(parts2)
    for axis in axes:
        reduce_start(1, axis, value)
        value = reduce_finish(1, axis)

    h1, h2, h3 = value, shift(value, -8), shift(value, -16)
    g1 = theta * own_gram + h1
    solved = eliminate(pack_lanes([g1, own_gram, h1]))
    alpha, rest = shift(solved, -8), shift(solved, -16)
    h1a, h2a = product(h1, alpha), product(h2, alpha)
    norm_next = product_t(rest, product(own_gram, rest) - h1a) + product_t(
        alpha, h2a - product(h1, rest)
    )
    beta = shift(eliminate(pack_lanes([own_gram, norm_next])), -8)
    mix = rest + beta
    cross = h2 + theta * h1
    curve = product_t(mix, product(g1, mix) - product(cross, alpha)) + product_t(
        alpha, product(h3, alpha) - product(cross, mix)
    )
    alpha2 = shift(eliminate(pack_lanes([curve, norm_next])), -8)
    second = product(alpha, alpha2)
    main = alpha + product(mix, alpha2) + theta * second
    c_out[pl.ds(0, 8)] = main
    c_out[pl.ds(8, 8)] = second

    store_q.wait()
    store_s.wait()
    for d in flat:
        sent_if(d, field_part(d, V, send1, recv1))
        sent_if(d, field_part(d, Q, send2, recv2))
    for d in flat_w:
        sent_if(d, weight_part(d))
    for d in cols:
        sent_if(d, column_part(d, True))
        sent_if(d, column_part(d, False))
    for which in range(2):
        for axis in axes:
            for copy in reduce_copies(which, axis):
                copy.wait_send()


def finish_kernel(c_ref, r_ref, q_ref, s_ref, x_out, r_out):
    planes = r_ref.shape[1]
    for j in range(N):
        main = [c_ref[i, j] for i in range(N)]
        second = [c_ref[N + i, j] for i in range(N)]

        def body(p, carry):
            for t in range(4):
                at = pl.ds(8 * t, 8)
                r = [r_ref[f, p, at] for f in range(N)]
                q = [q_ref[f, p, at] for f in range(N)]
                s = [s_ref[f, p, at] for f in range(N)]
                x = main[0] * r[0] - second[0] * q[0]
                res = second[0] * s[0] - main[0] * q[0]
                for i in range(1, N):
                    x = x + (main[i] * r[i] - second[i] * q[i])
                    res = res + (second[i] * s[i] - main[i] * q[i])
                x_out[j, p, at] = x
                r_out[j, p, at] = r[j] + res
            return carry

        lax.fori_loop(0, planes, body, 0)


def shards(sizes, rhs, stencil):
    nx, ny, nz = sizes
    block = rhs.shape
    anyspace = pl.BlockSpec(memory_space=pl.ANY)
    q, s, coef = pl.pallas_call(
        functools.partial(kernel, sizes),
        out_shape=(
            jax.ShapeDtypeStruct(block, F32),
            jax.ShapeDtypeStruct(block, F32),
            jax.ShapeDtypeStruct((16, 128), F32),
        ),
        in_specs=[anyspace, anyspace],
        out_specs=(anyspace, anyspace, pl.BlockSpec(memory_space=pltpu.VMEM)),
        scratch_shapes=[
            pltpu.VMEM((8, 18, 48, 128), F32),
            pltpu.VMEM((8, 18, 48, 128), F32),
            pltpu.VMEM((14, 17, 48, 128), F32),
            pltpu.VMEM((27, 16, 32, 128), F32),
            pltpu.VMEM((9, 16, 32, 128), F32),
            pltpu.VMEM((16, 32, 128), F32),
            pltpu.VMEM((2, 2, 32, 128), F32),
            pltpu.VMEM((2, 2, 4, 48, 128), F32),
            pltpu.VMEM((2, 32, 128), F32),
            pltpu.VMEM((2, 4, 48, 128), F32),
            pltpu.VMEM((18, 48, 128), F32),
            pltpu.VMEM((17, 48, 128), F32),
            pltpu.VMEM((8, 16, 32, 128), F32),
            pltpu.VMEM((2, 3, 8, 128), F32),
            pltpu.VMEM((2, nx + ny + nz, 8, 128), F32),
            pltpu.SemaphoreType.DMA((2,)),
            pltpu.SemaphoreType.DMA((2,)),
            pltpu.SemaphoreType.DMA((31,)),
            pltpu.SemaphoreType.DMA((31,)),
            pltpu.SemaphoreType.DMA((26,)),
            pltpu.SemaphoreType.DMA((26,)),
            pltpu.SemaphoreType.DMA((2, nx + ny + nz)),
            pltpu.SemaphoreType.DMA((2, nx + ny + nz)),
        ],
        compiler_params=pltpu.CompilerParams(
            collective_id=0, has_side_effects=True, vmem_limit_bytes=50 * 2**20
        ),
        name="operator",
    )(rhs, stencil)
    planes = 2
    spec = pl.BlockSpec((8, planes, 32, 128), lambda i: (0, i, 0, 0))
    return pl.pallas_call(
        finish_kernel,
        grid=(block[1] // planes,),
        out_shape=(jax.ShapeDtypeStruct(block, F32), jax.ShapeDtypeStruct(block, F32)),
        in_specs=[pl.BlockSpec(memory_space=pltpu.SMEM), spec, spec, spec],
        out_specs=(spec, spec),
        name="finish",
    )(coef[:, :8], rhs, q, s)


def solution(mesh):
    sizes = tuple(mesh.shape[n] for n in ("gx", "gy", "gz"))
    placed = P(None, "gx", "gy", "gz")
    return jax.shard_map(
        functools.partial(shards, sizes),
        mesh=mesh,
        in_specs=(placed, placed),
        out_specs=(placed, placed),
        check_vma=False,
    )
```

time: 396 us -> 72.9 us (0.18); the launches traced: 389 us -> 72.2 us
  other arithmetic: 107 us -> 0 us
  local copies, waits for them, and re-layouts: 95.3 us -> 1.89 us
  blocking collectives: 78.6 us -> 0 us
  Pallas kernels: 0 us -> 69.6 us
  starting transfers between devices: 49.6 us -> 0 us
  matrix products: 48.1 us -> 0 us
  waiting for transfers between devices: 8.57 us -> 0 us
    psum x8 -> x0, blocking collectives: 78.6 us -> none  [over_axes(): x = lax.psum(x, axis)]
    pallas_call x0 -> x2, Pallas kernels: none -> 69.6 us  [the longest x1 59.8 us: shards(): pl.pallas_call(functools.partial(kernel, sizes), out_shape=(jax.ShapeDtyp...]
    slice x51 -> x0, local copies, waits for them, and re-layouts: 61.5 us -> none  [the longest x35 28.2 us: window(): lax.slice_in_dim(result, begin, begin + inner + 2 * depth, axis=dim)]
    sub x2 -> x0, other arithmetic: 60.9 us -> none  [operate(): result = result - behind_w[None] * window(field, fmargin, depth, back)]
    ppermute x18 -> x0, starting transfers between devices: 49.6 us -> none  [the longest x9 33.5 us: with_halo(): lax.ppermute(tail, axis, [(i, (i + 1) % count) for i in range(ends)])]
    dot_general x14 -> x0, matrix products: 47 us -> none  [the longest x5 28.4 us: gram(): lax.dot_general(flat_l, flat_r, (((1,), (1,)), ((), ())), precision=lax.P...]
    concatenate x7 -> x0, other arithmetic: 34.9 us -> none  [with_halo(): jnp.concatenate([lax.ppermute(tail, axis, [(i, (i + 1) % count) for i in...]
    ppermute x8 -> x0, local copies, waits for them, and re-layouts: 19.4 us -> none  [the longest x4 9.74 us: with_halo(): lax.ppermute(head, axis, [((i + 1) % count, i) for i in range(ends)])]
  transfers between devices with their start and end apart: 18 -> 0, of which waited for: 3 -> 0; matrix products, arithmetic and copies ran while one was open for 16% -> 0% of each run, Pallas kernels for 0% -> 0%
where the time goes in v1:
time: 72.9 us; the launch traced here: 72.2 us
  Pallas kernels  69.6 us (95%)
  local copies, waits for them, and re-layouts  1.89 us (3%)
    pallas_call x1, Pallas kernels, shards(): pl.pallas_call(functools.partial(kernel, sizes), out_shape=(jax.ShapeDtyp...  59.8 us
    pallas_call x1, Pallas kernels, shards(): pl.pallas_call(finish_kernel, grid=(block[1] // planes,), out_shape=(jax....  9.86 us
    unnamed x4, local copies, waits for them, and re-layouts  1.89 us

profile of v1, /device:TPU:1, one launch (start us, length us, event | category | flops | bytes accessed | tf_op | source)
XLA Modules:
  0.0 72.2 jit_solution(3429085141297640489)
XLA Ops:
  0.6 59.8 %operator.1 = (f32[8,16,32,128]{3,2,1,0:T(8,128)S(1)}, f32[8,16,32,128]{3,2,1,0:T(8,128)}, f32[16,128]{1,0:T(8,128)S(1)}) custom-call(f32[8,16,32,128]{3,2,1,0:T(8,128)} %r_ref.1, f32[14,16,32,128]{3,2,1,0:T(8,128)} %w_ref.1), custom_call_target="tpu_custom_call" | custom-call | tf_op jit(solution)/shard_map/operator/pallas_call | solution.py:665
  60.4 0.0 copy-start
  60.4 1.3 %copy-done = f32[8,16,32,128]{3,2,1,0:T(8,128)} copy-done((f32[8,16,32,128]{3,2,1,0:T(8,128)}, f32[8,16,32,128]{3,2,1,0:T(8,128)S(1)}, u32[]{:S(2)}) %copy-start) | copy-done | bytes 2097176
  61.7 0.0 copy-start.1
  61.7 0.6 copy-done.1
  62.3 9.9 %finish.1 = (f32[8,16,32,128]{3,2,1,0:T(8,128)}, f32[8,16,32,128]{3,2,1,0:T(8,128)}) custom-call(f32[16,8]{1,0:T(8,128)} %bitcast.1, f32[8,16,32,128]{3,2,1,0:T(8,128)} %r_ref.1, f32[8,16,32,128]{3,2,1,0:T(8,128)} %copy-done, f32[8,16,32,128]{3,2,1,0:T(8,128)} %get-tuple-element.7.s_ref), custom_call_target="tpu_custom_call" | custom-call | tf_op jit(solution)/shard_map/finish/pallas_call | solution.py:706
Async XLA Ops:
  60.4 1.3 %copy-start = (f32[8,16,32,128]{3,2,1,0:T(8,128)}, f32[8,16,32,128]{3,2,1,0:T(8,128)S(1)}, u32[]{:S(2)}) copy-start(f32[8,16,32,128]{3,2,1,0:T(8,128)S(1)} %get-tuple-element.6.q_ref) | copy-start | bytes 6291460
  61.7 0.6 copy-start.1

commit v2 on v1

v2 whole, which is shorter than its diff:
```python
import functools

import jax
import jax.numpy as jnp
from jax import lax
from jax.experimental import pallas as pl
from jax.experimental.pallas import tpu as pltpu
from jax.sharding import PartitionSpec as P

F32 = jnp.float32
N = 8
FORWARD = [
    (a, b, c) for a in (-1, 0, 1) for b in (-1, 0, 1) for c in (-1, 0, 1) if (a, b, c) > (0, 0, 0)
]
INDEX = {o: k + 1 for k, o in enumerate(FORWARD)}
PLANE = [(a, b) for a in (-1, 0, 1) for b in (-1, 0, 1)]
SLOTS = [(0, 0), (0, 1), (1, -1), (1, 0), (1, 1)]
LOW = [INDEX[(a, b, 1)] for a, b in SLOTS]
UP = [INDEX[(a, b, -1)] if (a, b) != (0, 0) else INDEX[(0, 0, 1)] for a, b in SLOTS]
DIRS = [
    (a, b, c) for a in (-1, 0, 1) for b in (-1, 0, 1) for c in (-1, 0, 1) if (a, b, c) != (0, 0, 0)
]
WRANGE = {(1, 0): (5, 9), (1, 1): (11, 3), (1, -1): (5, 3), (0, 1): (2, 12), (0, -1): (5, 3)}
WDIRS = list(WRANGE)
PAIRS = [(i, j) for i in range(N) for j in range(i, N)]
TOP = 8


def lanes():
    return lax.broadcasted_iota(jnp.int32, (8, 128), 1)


def rows():
    return lax.broadcasted_iota(jnp.int32, (8, 128), 0)


def splat_row(m, k):
    return jnp.broadcast_to(m[k : k + 1, :], (8, 128))


def splat_col(m, k):
    return jnp.broadcast_to(m[:, k : k + 1], (8, 128))


def row_sum(m):
    return jnp.broadcast_to(jnp.sum(m, axis=1, keepdims=True), (8, 128))


def shift(m, amount):
    amount = amount % 128
    return pltpu.roll(m, amount, 1) if amount else m


def product(a, b):
    total = splat_col(a, 0) * splat_row(b, 0)
    for k in range(1, N):
        total = total + splat_col(a, k) * splat_row(b, k)
    return total


def product_t(a, b):
    same = lanes() == rows()
    total = None
    for k in range(N):
        column = row_sum(jnp.where(same, splat_row(a, k), 0.0))
        term = column * splat_row(b, k)
        total = term if total is None else total + term
    return total


def eliminate(m):
    row_id = rows()
    for k in range(N):
        pivot = splat_row(m, k)
        scaled = pivot / splat_col(pivot, k)
        m = jnp.where(row_id == k, scaled, m - splat_col(m, k) * scaled)
    return m


def pack_lanes(parts):
    lane = lanes()
    total = None
    for slot, part in enumerate(parts):
        here = (lane >= 8 * slot) & (lane < 8 * slot + 8)
        term = jnp.where(here, shift(part, 8 * slot), 0.0)
        total = term if total is None else total + term
    return total


def kernel(
    sizes,
    x_ref,
    w_ref,
    X1,
    R1,
    D2,
    A2,
    T,
    V,
    Q,
    S,
    TA,
    W,
    PX,
    WW,
    WE,
    R,
    PP,
    LPP,
    PQ,
    LPQ,
    G,
    GW,
    ARS,
    ARL,
    load_sem,
    send1,
    recv1,
    send2,
    recv2,
    ar_send,
    ar_recv,
):
    names = ("gx", "gy", "gz")
    nx, ny, nz = sizes
    me = tuple(lax.axis_index(n) for n in names)

    def exists(d):
        cond = None
        for pos, step, count in zip(me, d, sizes):
            term = None
            if step > 0:
                term = pos < count - 1
            elif step < 0:
                term = pos > 0
            if term is not None:
                cond = term if cond is None else cond & term
        return cond

    def opposite(d):
        return tuple(-t for t in d)

    def target(d):
        return tuple(pos + step for pos, step in zip(me, d))

    groups = ((1,), (0, 2))
    offsets = (
        [(0, p, 0) for p in range(1, ny)],
        [(p, 0, r) for p in range(nx) for r in range(nz) if p or r],
    )
    own_slot = (me[1], ny + me[0] * nz + me[2])
    slots = ((0, ny), (ny, nx * nz))

    def peer(d):
        return tuple(lax.rem(pos + p, n) if p else pos for pos, p, n in zip(me, d, sizes))

    load_x = pltpu.make_async_copy(x_ref, V.at[:, pl.ds(1, 16), pl.ds(TOP, 32)], load_sem.at[0])
    load_w = pltpu.make_async_copy(w_ref, W.at[:, pl.ds(1, 16), pl.ds(TOP, 32)], load_sem.at[1])
    load_x.start()
    load_w.start()

    zero = jnp.zeros((8, 128), F32)

    def clear_padded(buf, first, last):
        for field in range(buf.shape[0]):
            for plane in (first, last):
                if plane is not None:
                    for t in range(6):
                        buf[field, plane, pl.ds(8 * t, 8)] = zero

        def body(p, carry):
            for field in range(buf.shape[0]):
                buf[field, p, pl.ds(0, 8)] = zero
                buf[field, p, pl.ds(40, 8)] = zero
            return carry

        lax.fori_loop(1, 17, body, 0)

    clear_padded(V, 0, 17)
    clear_padded(Q, 0, 17)
    clear_padded(W, 0, None)

    def clear_landing(i, carry):
        for t in range(6):
            for s in range(2):
                for k in range(2):
                    LPP[s, k, i, pl.ds(8 * t, 8)] = zero
                LPQ[s, i, pl.ds(8 * t, 8)] = zero
        return carry

    lax.fori_loop(0, 4, clear_landing, 0)

    barrier = pltpu.get_barrier_semaphore()
    for d in DIRS:

        @pl.when(exists(d))
        def _():
            pl.semaphore_signal(
                barrier, inc=1, device_id=target(d), device_id_type=pl.DeviceIdType.MESH
            )

    for step in range(2):
        for d in offsets[step]:
            pl.semaphore_signal(
                barrier, inc=1, device_id=peer(d), device_id_type=pl.DeviceIdType.MESH
            )
    span = []
    for pos, count in zip(me, sizes):
        span.append(1 + (pos > 0).astype(jnp.int32) + (pos < count - 1).astype(jnp.int32))
    pl.semaphore_wait(
        barrier, span[0] * span[1] * span[2] - 1 + (ny - 1) + (nx * nz - 1)
    )

    def along(step, whole, plus, minus):
        if step == 0:
            return (pl.ds(*whole), pl.ds(*whole))
        src, dst = plus if step > 0 else minus
        return (pl.ds(src, 1), pl.ds(dst, 1))

    def field_part(d, buf, sends, recvs):
        i = DIRS.index(d)
        xs, xd = along(d[0], (1, 16), (16, 0), (1, 17))
        ys, yd = along(d[1], (TOP, 32), (TOP + 31, TOP - 1), (TOP, TOP + 32))
        return pltpu.make_async_remote_copy(
            src_ref=buf.at[:, xs, ys],
            dst_ref=buf.at[:, xd, yd],
            send_sem=sends.at[i],
            recv_sem=recvs.at[i],
            device_id=target(d),
            device_id_type=pl.DeviceIdType.MESH,
        )

    def weight_part(d):
        i = 26 + WDIRS.index((d[0], d[1]))
        k0, kn = WRANGE[(d[0], d[1])]
        xs, xd = along(d[0], (1, 16), (16, 0), (1, 17))
        ys, yd = along(d[1], (TOP, 32), (TOP + 31, TOP - 1), (TOP, TOP + 32))
        return pltpu.make_async_remote_copy(
            src_ref=W.at[pl.ds(k0, kn), xs, ys],
            dst_ref=W.at[pl.ds(k0, kn), xd, yd],
            send_sem=send1.at[i],
            recv_sem=recv1.at[i],
            device_id=target(d),
            device_id_type=pl.DeviceIdType.MESH,
        )

    def column_part(d, both):
        i = DIRS.index(d)
        side = 0 if d[2] > 0 else 1
        if d[0] == 0:
            gs, gd = pl.ds(0, 2), pl.ds(1, 2)
        elif d[0] > 0:
            gs, gd = pl.ds(1, 1), pl.ds(0, 1)
        else:
            gs, gd = pl.ds(0, 1), pl.ds(3, 1)
        if d[1] == 0:
            ys, yd = pl.ds(0, 32), pl.ds(TOP, 32)
        elif d[1] > 0:
            ys, yd = pl.ds(31, 1), pl.ds(TOP - 1, 1)
        else:
            ys, yd = pl.ds(0, 1), pl.ds(TOP + 32, 1)
        src = PP.at[:, gs, ys] if both else PQ.at[gs, ys]
        dst = LPP.at[side, :, gd, yd] if both else LPQ.at[side, gd, yd]
        return pltpu.make_async_remote_copy(
            src_ref=src,
            dst_ref=dst,
            send_sem=(send1 if both else send2).at[i],
            recv_sem=(recv1 if both else recv2).at[i],
            device_id=target(d),
            device_id_type=pl.DeviceIdType.MESH,
        )

    def start_if(d, copy):
        @pl.when(exists(d))
        def _():
            copy.start()

    def recv_if(d, copy):
        @pl.when(exists(opposite(d)))
        def _():
            copy.wait_recv()

    def sent_if(d, copy):
        @pl.when(exists(d))
        def _():
            copy.wait_send()

    flat = sorted((d for d in DIRS if d[2] == 0), key=lambda d: abs(d[1]))
    flat_w = [(a, b, 0) for a, b in WDIRS]
    cols = [d for d in DIRS if d[2] != 0]

    lane = lanes()
    odd = lax.rem(lane, 2) == 1
    first = lane == 0
    last = lane == 127
    half = lane // 2

    def gather_columns(fields):
        total = zero
        for slot, v in enumerate(fields):
            total = jnp.where(half == slot, shift(v, 2 * slot + 1), total)
        return total

    def merge_columns(dst):
        def body(xg, carry):
            for t in range(4):
                at = pl.ds(8 * t, 8)
                parts = [
                    jnp.where(lane // 16 == xm, shift(PX[xg * 8 + xm, at], 16 * xm), 0.0)
                    for xm in range(8)
                ]
                while len(parts) > 1:
                    parts = [a + b for a, b in zip(parts[::2], parts[1::2])]
                dst(xg, at, parts[0])
            return carry

        lax.fori_loop(0, 2, body, 0)

    def pack(dst, group):
        def body(x, carry):
            for t in range(4):
                PX[x, pl.ds(8 * t, 8)] = gather_columns(
                    group(x + 1, pl.ds(TOP + 8 * t, 8))
                )
            return carry

        lax.fori_loop(0, 16, body, 0)
        merge_columns(dst)

    def put_weights(xg, at, total):
        PP[1, xg, at] = total

    def weight_group(p, at):
        return [jnp.where(first, W[UP[j], p, at], W[LOW[j], p, at]) for j in range(5)]

    def unpack(get, dst, planes):
        def body(t, carry):
            r0 = pl.multiple_of(8 * t, 8)
            merged = {}
            for xi in planes:
                if xi == 0:
                    g, off = 0, 112
                elif xi == 17:
                    g, off = 3, 0
                else:
                    g, off = 1 + (xi - 1) // 8, 16 * ((xi - 1) % 8)
                if g not in merged:
                    merged[g] = jnp.where(odd, get(1, g, r0), get(0, g, r0))
                dst[xi, pl.ds(r0, 8)] = shift(merged[g], -off)
            return carry

        lax.fori_loop(0, 6, body, 0)

    flat_y = [d for d in flat if d[0] == 0]
    flat_x = [d for d in flat if d[0] != 0]
    flat_wy = [d for d in flat_w if d[0] == 0]
    flat_wx = [d for d in flat_w if d[0] != 0]
    cols_y = [d for d in cols if d[0] == 0]
    cols_x = [d for d in cols if d[0] != 0]

    load_x.wait()
    for d in flat_y + flat_x:
        start_if(d, field_part(d, V, send1, recv1))

    def put_pp(xg, at, total):
        PP[0, xg, at] = total

    pack(put_pp, lambda p, at: [V[f, p, at] for f in range(N)])
    load_w.wait()
    for d in flat_wy:
        start_if(d, weight_part(d))
    pack(put_weights, weight_group)
    for d in cols_y + cols_x:
        start_if(d, column_part(d, True))
    for d in flat_wx:
        start_if(d, weight_part(d))

    def m_of(a, b):
        return 3 * (a + 1) + (b + 1)

    def spread_columns(v, even_from, odd_from):
        return jnp.take_along_axis(v, jnp.where(odd, odd_from, even_from), axis=1)

    def prepare_own(x, carry):
        for t in range(4):
            out = pl.ds(8 * t, 8)
            own = [W[k, x + 1, pl.ds(TOP + 8 * t, 8)] for k in range(14)]
            diag = (own[0] + own[1]) + (own[2] + own[3])
            for k in range(4, 14, 2):
                diag = diag + (own[k] + own[k + 1])
            WW[0, x, out] = diag
            for j, (a, b) in enumerate(SLOTS):
                WW[1 + j, x, out] = shift(own[LOW[j]], 1)
                if j:
                    WW[5 + j, x, out] = shift(own[UP[j]], 127)
                    WE[m_of(a, b), x, out] = spread_columns(
                        jnp.where(first, own[UP[j]], own[LOW[j]]), 0, 127
                    )
        return carry

    def prepare(x, carry):
        for t in range(4):
            r0 = TOP + 8 * t

            def w_at(k, a=0, b=0):
                return W[k, x + 1 + a, pl.ds(r0 + b, 8)]

            out = pl.ds(8 * t, 8)
            diag = WW[0, x, out]
            ahead = zero
            behind = w_at(LOW[0])
            own = spread_columns(
                jnp.where(last, behind, GW[x + 1, pl.ds(r0, 8)]), 0, 127
            )
            WE[m_of(0, 0), x, out] = own
            edge = jnp.where(odd, 0.0, own)
            for j, (a, b) in enumerate(SLOTS):
                if j == 0:
                    continue
                back = spread_columns(GW[x + 1 - a, pl.ds(r0 - b, 8)], 2 * j, 2 * j + 1)
                WE[m_of(-a, -b), x, out] = back
                edge = edge + back
                diag = diag + w_at(INDEX[(a, b, 0)], -a, -b)
                ahead = ahead + w_at(UP[j], -a, -b)
                behind = behind + w_at(LOW[j], -a, -b)
            diag = diag + jnp.where(last, edge, shift(ahead, 127))
            diag = diag + jnp.where(first, edge, shift(behind, 1))
            WW[0, x, out] = diag
        return carry

    lax.fori_loop(0, 16, prepare_own, 0)

    def gram_loop(get):
        sums = []
        for lo, hi in ((0, 3), (3, N)):
            pairs = [(i, j) for i, j in PAIRS if lo <= i < hi]

            def body(x, acc):
                acc = list(acc)
                for t in range(4):
                    left, right = get(x, t, range(lo, hi), range(lo, N))
                    for n, (i, j) in enumerate(pairs):
                        acc[n] = acc[n] + left[i] * right[j]
                return tuple(acc)

            sums += list(lax.fori_loop(0, 16, body, tuple(zero for _ in pairs)))
        return sums

    def spread(parts, acc, offset):
        for n, (i, j) in enumerate(PAIRS):
            total = row_sum(acc[n])
            parts[i] = jnp.where(lane == offset + j, total, parts[i])
            if i != j:
                parts[j] = jnp.where(lane == offset + i, total, parts[j])
        return parts

    def fold(parts):
        result = zero
        for i in range(N):
            total = jnp.broadcast_to(jnp.sum(parts[i], axis=0, keepdims=True), (8, 128))
            result = jnp.where(rows() == i, total, result)
        return result

    def row(buf, f, x, t):
        return buf[f, x + 1, pl.ds(TOP + 8 * t, 8)]

    def get_rr(x, t, left, right):
        v = {f: row(V, f, x, t) for f in right}
        return v, v

    parts1 = spread([zero] * N, gram_loop(get_rr), 0)

    for d in flat_y:
        recv_if(d, field_part(d, V, send1, recv1))
    for d in flat_wy:
        recv_if(d, weight_part(d))
    for d in cols_y:
        recv_if(d, column_part(d, True))

    def get_lpp(k):
        return lambda s, g, r0: LPP[s, k, g, pl.ds(r0, 8)]

    def get_lpq(s, g, r0):
        return LPQ[s, g, pl.ds(r0, 8)]

    unpack(get_lpp(0), G, range(1, 17))
    unpack(get_lpp(1), GW, range(1, 17))

    def edges(x, carry):
        for t in range(4):
            total = zero
            for a, b in PLANE:
                total = total + WE[m_of(a, b), x, pl.ds(8 * t, 8)] * G[
                    x + 1 + a, pl.ds(TOP + 8 * t + b, 8)
                ]
            R[x, pl.ds(8 * t, 8)] = total
        return carry

    def coupling(x, t, a, b, c):
        j = SLOTS.index((a, b)) if (a, b) in SLOTS else SLOTS.index((-a, -b))
        here = pl.ds(8 * t, 8)
        away = W.at[:, x + 1 + a, pl.ds(TOP + 8 * t + b, 8)]
        ahead = (a, b) in SLOTS
        if c == 0:
            if (a, b) == (0, 0):
                return WW[0, x, here]
            if ahead:
                return W[INDEX[(a, b, 0)], x + 1, pl.ds(TOP + 8 * t, 8)]
            return away[INDEX[(-a, -b, 0)]]
        if c == 1:
            return WW[1 + j, x, here] if ahead else away[UP[j]]
        if ahead and j:
            return WW[5 + j, x, here]
        return away[LOW[j]]

    def operate(src, put, pack_too=False):
        def body(x, carry):
            for t in range(4):
                weights = [
                    [coupling(x, t, a, b, c) for a, b in PLANE] for c in (0, 1, -1)
                ]
                halo = R[x, pl.ds(8 * t, 8)]
                columns = zero
                for f in range(N):
                    sums = [None, None, None]
                    for m, (a, b) in enumerate(PLANE):
                        v = src[f, x + 1 + a, pl.ds(TOP + 8 * t + b, 8)]
                        if (a, b) == (0, 0):
                            centre = weights[0][m] * v
                        for c in range(3):
                            if c == 0 and (a, b) == (0, 0):
                                continue
                            term = weights[c][m] * v
                            sums[c] = term if sums[c] is None else sums[c] + term
                    side = shift(halo, -(2 * f + 1))
                    total = centre - sums[0]
                    total = total - shift(jnp.where(first, side, sums[1]), 127)
                    total = total - shift(jnp.where(last, side, sums[2]), 1)
                    put(f, x, t, total)
                    if pack_too:
                        columns = jnp.where(half == f, shift(total, 2 * f + 1), columns)
                if pack_too:
                    PX[x, pl.ds(8 * t, 8)] = columns
            return carry

        return body

    def ends(body):
        return lambda i, carry: body(15 * i, carry)

    def put_q(f, x, t, value):
        Q[f, x + 1, pl.ds(TOP + 8 * t, 8)] = value

    def put_s(f, x, t, value):
        S[f, x, pl.ds(8 * t, 8)] = value

    lax.fori_loop(1, 16, prepare, 0)
    lax.fori_loop(1, 15, edges, 0)
    lax.fori_loop(1, 15, operate(V, put_q, True), 0)
    for d in flat_x:
        recv_if(d, field_part(d, V, send1, recv1))
    for d in flat_wx:
        recv_if(d, weight_part(d))
    for d in cols_x:
        recv_if(d, column_part(d, True))
    unpack(get_lpp(0), G, (0, 17))
    unpack(get_lpp(1), GW, (0,))
    prepare(0, 0)
    lax.fori_loop(0, 2, ends(edges), 0)
    lax.fori_loop(0, 2, ends(operate(V, put_q, True)), 0)

    for d in flat_y + flat_x:
        start_if(d, field_part(d, Q, send2, recv2))

    def put_pq(xg, at, total):
        PQ[xg, at] = total

    merge_columns(put_pq)
    for d in cols_y + cols_x:
        start_if(d, column_part(d, False))

    def reduce_copies(which, step):
        copies = []
        for i, d in enumerate(offsets[step]):
            i = slots[step][0] + i
            copies.append(
                pltpu.make_async_remote_copy(
                    src_ref=ARS.at[which, step],
                    dst_ref=ARL.at[which, own_slot[step]],
                    send_sem=ar_send.at[which, i],
                    recv_sem=ar_recv.at[which, i],
                    device_id=peer(d),
                    device_id_type=pl.DeviceIdType.MESH,
                )
            )
        return copies

    def reduce_start(which, step, value):
        ARS[which, step] = value
        ARL[which, own_slot[step]] = value
        for copy in reduce_copies(which, step):
            copy.start()

    def reduce_finish(which, step):
        for copy in reduce_copies(which, step):
            copy.wait_recv()
        lo, count = slots[step]
        parts = [ARL[which, lo + i] for i in range(count)]
        while len(parts) > 1:
            parts = [a + b for a, b in zip(parts[::2], parts[1::2])]
        return parts[0]

    def get_rq(x, t, left, right):
        return (
            {f: row(V, f, x, t) for f in left},
            {f: row(Q, f, x, t) for f in right},
        )

    def get_qq(x, t, left, right):
        q = {f: row(Q, f, x, t) for f in right}
        return q, q

    parts1 = spread(parts1, gram_loop(get_rq), 8)
    parts1 = spread(parts1, gram_loop(get_qq), 16)
    reduce_start(0, 0, fold(parts1))

    for d in flat_y:
        recv_if(d, field_part(d, Q, send2, recv2))
    for d in cols_y:
        recv_if(d, column_part(d, False))
    unpack(get_lpq, G, range(1, 17))
    lax.fori_loop(1, 15, edges, 0)
    lax.fori_loop(1, 5, operate(Q, put_s), 0)
    reduce_start(0, 1, reduce_finish(0, 0))
    lax.fori_loop(5, 15, operate(Q, put_s), 0)
    for d in flat_x:
        recv_if(d, field_part(d, Q, send2, recv2))
    for d in cols_x:
        recv_if(d, column_part(d, False))
    unpack(get_lpq, G, (0, 17))
    lax.fori_loop(0, 2, ends(edges), 0)
    lax.fori_loop(0, 2, ends(operate(Q, put_s)), 0)
    sum1 = reduce_finish(0, 1)

    def trace(m):
        total = row_sum(jnp.where(lane == rows(), m, 0.0))
        return jnp.broadcast_to(jnp.sum(total, axis=0, keepdims=True), (8, 128))

    small = lane < 8
    own_gram = jnp.where(small, sum1, 0.0)
    g1 = jnp.where(small, shift(sum1, -8), 0.0)
    g2 = shift(sum1, -16)
    theta = trace(g1) / trace(own_gram)
    h1 = g1 - theta * own_gram

    def moved(f, x, t):
        return row(Q, f, x, t) - theta * row(V, f, x, t)

    def get_h2(x, t, left, right):
        z = {f: moved(f, x, t) for f in right}
        return z, z

    def get_zs(x, t, left, right):
        return (
            {f: moved(f, x, t) for f in left},
            {f: S[f, x, pl.ds(8 * t, 8)] for f in right},
        )

    parts2 = [zero] * N
    parts2 = spread(parts2, gram_loop(get_h2), 0)
    parts2 = spread(parts2, gram_loop(get_zs), 8)
    reduce_start(1, 0, fold(parts2))

    unit = jnp.where(lane == rows(), 1.0, 0.0)
    solved = eliminate(pack_lanes([g1, own_gram, h1]))
    inverse = shift(eliminate(pack_lanes([own_gram, unit])), -8)
    alpha, rest = shift(solved, -8), shift(solved, -16)
    beta = own_gram - product(g1, alpha) + product_t(alpha, product(g2, alpha) - g1)
    beta = product(inverse, beta)
    mix = rest + beta
    early = product(own_gram, rest) - product(h1, alpha)
    early = product_t(rest, early) - product_t(alpha, product(h1, rest))

    def put_table(dst, base, m):
        for i in range(N):
            line = splat_row(m, i)
            for j in range(N):
                dst[base + N * j + i] = splat_col(line, j)

    put_table(TA, 0, alpha)
    put_table(TA, 64, unit + beta)

    def second_body(j, carry):
        a = [TA[N * j + i] for i in range(N)]
        b = [TA[64 + N * j + i] for i in range(N)]

        def body(x, carry):
            for t in range(4):
                at = pl.ds(8 * t, 8)
                r = [row(V, f, x, t) for f in range(N)]
                q = [row(Q, f, x, t) for f in range(N)]
                s = [S[f, x, at] for f in range(N)]

                def comb(c, v):
                    total = c[0] * v[0]
                    for i in range(1, N):
                        total = total + c[i] * v[i]
                    return total

                aq = comb(a, q)
                X1[j, x, at] = comb(a, r)
                R1[j, x, at] = row(V, j, x, t) - aq
                D2[j, x, at] = comb(b, r) - aq
                A2[j, x, at] = comb(b, q) - comb(a, s)
            return carry

        lax.fori_loop(0, 16, body, 0)
        return carry

    lax.fori_loop(0, 2, second_body, 0)
    reduce_start(1, 1, reduce_finish(1, 0))
    lax.fori_loop(2, N, second_body, 0)
    sum2 = reduce_finish(1, 1)

    h2, zs = sum2, shift(sum2, -8)
    norm_next = early + product_t(alpha, product(h2, alpha))
    cross = h2 + theta * h1
    h3 = zs - theta * cross
    curve = product_t(mix, product(g1, mix) - product(cross, alpha)) + product_t(
        alpha, product(h3, alpha) - product(cross, mix)
    )
    alpha2 = shift(eliminate(pack_lanes([curve, norm_next])), -8)
    put_table(T, 0, alpha2)

    for d in flat:
        sent_if(d, field_part(d, V, send1, recv1))
        sent_if(d, field_part(d, Q, send2, recv2))
    for d in flat_w:
        sent_if(d, weight_part(d))
    for d in cols:
        sent_if(d, column_part(d, True))
        sent_if(d, column_part(d, False))
    for which in range(2):
        for step in range(2):
            for copy in reduce_copies(which, step):
                copy.wait_send()


def finish_kernel(X1, R1, D2, A2, T, x_out, r_out, X, Y, sems):
    def store(j):
        return [
            pltpu.make_async_copy(buf.at[j], out.at[j], sems.at[k, j])
            for k, (buf, out) in enumerate(((X, x_out), (Y, r_out)))
        ]

    for j in range(N):
        a = [T[N * j + i] for i in range(N)]

        def body(p, carry):
            for t in range(4):
                at = pl.ds(8 * t, 8)
                x = X1[j, p, at]
                res = R1[j, p, at]
                for i in range(0, N, 2):
                    x = x + (a[i] * D2[i, p, at] + a[i + 1] * D2[i + 1, p, at])
                    res = res - (a[i] * A2[i, p, at] + a[i + 1] * A2[i + 1, p, at])
                X[j, p, at] = x
                Y[j, p, at] = res
            return carry

        lax.fori_loop(0, 16, body, 0)
        for copy in store(j):
            copy.start()
    for j in range(N):
        for copy in store(j):
            copy.wait()


def shards(sizes, rhs, stencil):
    nx, ny, nz = sizes
    block = rhs.shape
    anyspace = pl.BlockSpec(memory_space=pl.ANY)
    local = pl.BlockSpec(memory_space=pltpu.VMEM)
    hbm = pl.BlockSpec(memory_space=pltpu.HBM)
    field = jax.ShapeDtypeStruct(block, F32)
    kept = pl.pallas_call(
        functools.partial(kernel, sizes),
        out_shape=(field,) * 4 + (jax.ShapeDtypeStruct((64, 8, 128), F32),),
        in_specs=[hbm, hbm],
        out_specs=(local,) * 5,
        scratch_shapes=[
            pltpu.VMEM((8, 18, 48, 128), F32),
            pltpu.VMEM((8, 18, 48, 128), F32),
            pltpu.VMEM(block, F32),
            pltpu.VMEM((128, 8, 128), F32),
            pltpu.VMEM((14, 17, 48, 128), F32),
            pltpu.VMEM((16, 32, 128), F32),
            pltpu.VMEM((10, 16, 32, 128), F32),
            pltpu.VMEM((9, 16, 32, 128), F32),
            pltpu.VMEM((16, 32, 128), F32),
            pltpu.VMEM((2, 2, 32, 128), F32),
            pltpu.VMEM((2, 2, 4, 48, 128), F32),
            pltpu.VMEM((2, 32, 128), F32),
            pltpu.VMEM((2, 4, 48, 128), F32),
            pltpu.VMEM((18, 48, 128), F32),
            pltpu.VMEM((17, 48, 128), F32),
            pltpu.VMEM((2, 2, 8, 128), F32),
            pltpu.VMEM((2, ny + nx * nz, 8, 128), F32),
            pltpu.SemaphoreType.DMA((2,)),
            pltpu.SemaphoreType.DMA((31,)),
            pltpu.SemaphoreType.DMA((31,)),
            pltpu.SemaphoreType.DMA((26,)),
            pltpu.SemaphoreType.DMA((26,)),
            pltpu.SemaphoreType.DMA((2, ny + nx * nz)),
            pltpu.SemaphoreType.DMA((2, ny + nx * nz)),
        ],
        compiler_params=pltpu.CompilerParams(
            collective_id=0, has_side_effects=True, vmem_limit_bytes=44 * 2**20
        ),
        name="operator",
    )(rhs, stencil)
    return pl.pallas_call(
        finish_kernel,
        out_shape=(jax.ShapeDtypeStruct(block, F32), jax.ShapeDtypeStruct(block, F32)),
        in_specs=[local] * 5,
        out_specs=(anyspace, anyspace),
        scratch_shapes=[
            pltpu.VMEM(block, F32),
            pltpu.VMEM(block, F32),
            pltpu.SemaphoreType.DMA((2, N)),
        ],
        compiler_params=pltpu.CompilerParams(vmem_limit_bytes=24 * 2**20),
        name="finish",
    )(*kept)


def solution(mesh):
    sizes = tuple(mesh.shape[n] for n in ("gx", "gy", "gz"))
    placed = P(None, "gx", "gy", "gz")
    return jax.shard_map(
        functools.partial(shards, sizes),
        mesh=mesh,
        in_specs=(placed, placed),
        out_specs=(placed, placed),
        check_vma=False,
    )
```

time: 72.9 us -> 59.1 us (0.81)
  Pallas kernels: 69.6 us -> 58.4 us
  local copies, waits for them, and re-layouts: 1.89 us -> 0 us
    pallas_call x2, Pallas kernels: 69.6 us -> 58.4 us  [the longest x1 54.3 us: shards(): pl.pallas_call(functools.partial(kernel, sizes), out_shape=(field,) * 4 +...]
    unnamed x4 -> x0, local copies, waits for them, and re-layouts: 1.89 us -> none
where the time goes in v2:
time: 59.1 us; the launch traced here: 59 us
  Pallas kernels  58.4 us (99%)
  between operations  0.64 us (1%)
    pallas_call x1, Pallas kernels, shards(): pl.pallas_call(functools.partial(kernel, sizes), out_shape=(field,) * 4 +...  54.3 us
    pallas_call x1, Pallas kernels, shards(): pl.pallas_call(finish_kernel, out_shape=(jax.ShapeDtypeStruct(block, F32)...  4.1 us

profile of v2, /device:TPU:1, one launch (start us, length us, event | category | flops | bytes accessed | tf_op | source)
XLA Modules:
  0.0 59.0 jit_solution(4820420563410622002)
XLA Ops:
  0.6 54.3 %operator.1 = (f32[8,16,32,128]{3,2,1,0:T(8,128)S(1)}, f32[8,16,32,128]{3,2,1,0:T(8,128)S(1)}, f32[8,16,32,128]{3,2,1,0:T(8,128)S(1)}, f32[8,16,32,128]{3,2,1,0:T(8,128)S(1)}, f32[64,8,128]{2,1,0:T(8,128)S(1)}) custom-call(f32[8,16,32,128]{3,2,1,0:T(8,128)} %x_ref.1, f32[14,16,32,128]{3,2,1,0:T(8,128)} %w_ref.1), custom_call_target="tpu_custom_call" | custom-call | tf_op jit(solution)/shard_map/operator/pallas_call | solution.py:786
  54.9 4.1 %finish.1 = (f32[8,16,32,128]{3,2,1,0:T(8,128)}, f32[8,16,32,128]{3,2,1,0:T(8,128)}) custom-call(f32[8,16,32,128]{3,2,1,0:T(8,128)S(1)} %get-tuple-element.7.X1, f32[8,16,32,128]{3,2,1,0:T(8,128)S(1)} %get-tuple-element.8.R1, f32[8,16,32,128]{3,2,1,0:T(8,128)S(1)} %get-tuple-element.9.D2, f32[8,16,32,128]{3,2,1,0:T(8,128)S(1)} %get-tuple-element.10.A2, ...), custom_call_target="tpu_custom_call" | custom-call | tf_op jit(solution)/shard_map/finish/pallas_call | solution.py:822

commit v3 on v2

--- a/solution.py
+++ b/solution.py
@@ -51,40 +51,37 @@
     return pltpu.roll(m, amount, 1) if amount else m
 
 
-def product(a, b):
-    total = splat_col(a, 0) * splat_row(b, 0)
-    for k in range(1, N):
-        total = total + splat_col(a, k) * splat_row(b, k)
-    return total
-
-
-def product_t(a, b):
+def columns(m, base=0):
+    return [splat_col(m, base + k) for k in range(N)]
+
+
+def columns_t(m):
     same = lanes() == rows()
-    total = None
-    for k in range(N):
-        column = row_sum(jnp.where(same, splat_row(a, k), 0.0))
-        term = column * splat_row(b, k)
-        total = term if total is None else total + term
-    return total
-
-
-def eliminate(m):
+    return [row_sum(jnp.where(same, splat_row(m, k), 0.0)) for k in range(N)]
+
+
+def times(cols, m):
+    terms = [cols[k] * splat_row(m, k) for k in range(N)]
+    while len(terms) > 1:
+        terms = [a + b for a, b in zip(terms[::2], terms[1::2])]
+    return terms[0]
+
+
+def solve(cols, rights):
+    cols = list(cols)
     row_id = rows()
     for k in range(N):
-        pivot = splat_row(m, k)
-        scaled = pivot / splat_col(pivot, k)
-        m = jnp.where(row_id == k, scaled, m - splat_col(m, k) * scaled)
-    return m
-
-
-def pack_lanes(parts):
-    lane = lanes()
-    total = None
-    for slot, part in enumerate(parts):
-        here = (lane >= 8 * slot) & (lane < 8 * slot + 8)
-        term = jnp.where(here, shift(part, 8 * slot), 0.0)
-        total = term if total is None else total + term
-    return total
+        here = row_id == k
+        inverse = 1.0 / splat_row(cols[k], k)
+        factor = cols[k] * inverse
+
+        def step(m):
+            line = splat_row(m, k)
+            return jnp.where(here, line * inverse, m - factor * line)
+
+        cols = cols[: k + 1] + [step(c) for c in cols[k + 1 :]]
+        rights = [step(r) for r in rights]
+    return rights
 
 
 def kernel(
@@ -207,10 +204,6 @@
     span = []
     for pos, count in zip(me, sizes):
         span.append(1 + (pos > 0).astype(jnp.int32) + (pos < count - 1).astype(jnp.int32))
-    pl.semaphore_wait(
-        barrier, span[0] * span[1] * span[2] - 1 + (ny - 1) + (nx * nz - 1)
-    )
-
     def along(step, whole, plus, minus):
         if step == 0:
             return (pl.ds(*whole), pl.ds(*whole))
@@ -302,7 +295,7 @@
         return total
 
     def merge_columns(dst):
-        def body(xg, carry):
+        for xg in range(2):
             for t in range(4):
                 at = pl.ds(8 * t, 8)
                 parts = [
@@ -312,19 +305,18 @@
                 while len(parts) > 1:
                     parts = [a + b for a, b in zip(parts[::2], parts[1::2])]
                 dst(xg, at, parts[0])
+
+    def pack(dst, group):
+        def body(i, carry):
+            for k in range(4):
+                x = 4 * i + k
+                for t in range(4):
+                    PX[x, pl.ds(8 * t, 8)] = gather_columns(
+                        group(x + 1, pl.ds(TOP + 8 * t, 8))
+                    )
             return carry
 
-        lax.fori_loop(0, 2, body, 0)
-
-    def pack(dst, group):
-        def body(x, carry):
-            for t in range(4):
-                PX[x, pl.ds(8 * t, 8)] = gather_columns(
-                    group(x + 1, pl.ds(TOP + 8 * t, 8))
-                )
-            return carry
-
-        lax.fori_loop(0, 16, body, 0)
+        lax.fori_loop(0, 4, body, 0)
         merge_columns(dst)
 
     def put_weights(xg, at, total):
@@ -334,8 +326,8 @@
         return [jnp.where(first, W[UP[j], p, at], W[LOW[j], p, at]) for j in range(5)]
 
     def unpack(get, dst, planes):
-        def body(t, carry):
-            r0 = pl.multiple_of(8 * t, 8)
+        for t in range(6):
+            r0 = 8 * t
             merged = {}
             for xi in planes:
                 if xi == 0:
@@ -347,9 +339,14 @@
                 if g not in merged:
                     merged[g] = jnp.where(odd, get(1, g, r0), get(0, g, r0))
                 dst[xi, pl.ds(r0, 8)] = shift(merged[g], -off)
+
+    def blocks(body, first_x, count, width):
+        def several(i, carry):
+            for k in range(width):
+                body(first_x + width * i + k, carry)
             return carry
 
-        lax.fori_loop(0, 6, body, 0)
+        lax.fori_loop(0, count, several, 0)
 
     flat_y = [d for d in flat if d[0] == 0]
     flat_x = [d for d in flat if d[0] != 0]
@@ -358,19 +355,27 @@
     cols_y = [d for d in cols if d[0] == 0]
     cols_x = [d for d in cols if d[0] != 0]
 
-    load_x.wait()
-    for d in flat_y + flat_x:
-        start_if(d, field_part(d, V, send1, recv1))
-
     def put_pp(xg, at, total):
         PP[0, xg, at] = total
 
+    load_x.wait()
     pack(put_pp, lambda p, at: [V[f, p, at] for f in range(N)])
     load_w.wait()
+    pack(put_weights, weight_group)
+
+    pl.semaphore_wait(
+        barrier, span[0] * span[1] * span[2] - 1 + (ny - 1) + (nx * nz - 1)
+    )
+
+    for d in flat_y:
+        start_if(d, field_part(d, V, send1, recv1))
     for d in flat_wy:
         start_if(d, weight_part(d))
-    pack(put_weights, weight_group)
-    for d in cols_y + cols_x:
+    for d in cols_y:
+        start_if(d, column_part(d, True))
+    for d in flat_x:
+        start_if(d, field_part(d, V, send1, recv1))
+    for d in cols_x:
         start_if(d, column_part(d, True))
     for d in flat_wx:
         start_if(d, weight_part(d))
@@ -428,7 +433,7 @@
             WW[0, x, out] = diag
         return carry
 
-    lax.fori_loop(0, 16, prepare_own, 0)
+    blocks(prepare_own, 0, 8, 2)
 
     def gram_loop(get):
         sums = []
@@ -513,14 +518,13 @@
             return WW[5 + j, x, here]
         return away[LOW[j]]
 
-    def operate(src, put, pack_too=False):
+    def operate(src, put):
         def body(x, carry):
             for t in range(4):
                 weights = [
                     [coupling(x, t, a, b, c) for a, b in PLANE] for c in (0, 1, -1)
                 ]
                 halo = R[x, pl.ds(8 * t, 8)]
-                columns = zero
                 for f in range(N):
                     sums = [None, None, None]
                     for m, (a, b) in enumerate(PLANE):
@@ -537,10 +541,6 @@
                     total = total - shift(jnp.where(first, side, sums[1]), 127)
                     total = total - shift(jnp.where(last, side, sums[2]), 1)
                     put(f, x, t, total)
-                    if pack_too:
-                        columns = jnp.where(half == f, shift(total, 2 * f + 1), columns)
-                if pack_too:
-                    PX[x, pl.ds(8 * t, 8)] = columns
             return carry
 
         return body
@@ -554,9 +554,9 @@
     def put_s(f, x, t, value):
         S[f, x, pl.ds(8 * t, 8)] = value
 
-    lax.fori_loop(1, 16, prepare, 0)
+    blocks(prepare, 1, 5, 3)
     lax.fori_loop(1, 15, edges, 0)
-    lax.fori_loop(1, 15, operate(V, put_q, True), 0)
+    lax.fori_loop(1, 15, operate(V, put_q), 0)
     for d in flat_x:
         recv_if(d, field_part(d, V, send1, recv1))
     for d in flat_wx:
@@ -567,7 +567,7 @@
     unpack(get_lpp(1), GW, (0,))
     prepare(0, 0)
     lax.fori_loop(0, 2, ends(edges), 0)
-    lax.fori_loop(0, 2, ends(operate(V, put_q, True)), 0)
+    lax.fori_loop(0, 2, ends(operate(V, put_q)), 0)
 
     for d in flat_y + flat_x:
         start_if(d, field_part(d, Q, send2, recv2))
@@ -575,7 +575,7 @@
     def put_pq(xg, at, total):
         PQ[xg, at] = total
 
-    merge_columns(put_pq)
+    pack(put_pq, lambda p, at: [Q[f, p, at] for f in range(N)])
     for d in cols_y + cols_x:
         start_if(d, column_part(d, False))
 
@@ -672,14 +672,18 @@
     reduce_start(1, 0, fold(parts2))
 
     unit = jnp.where(lane == rows(), 1.0, 0.0)
-    solved = eliminate(pack_lanes([g1, own_gram, h1]))
-    inverse = shift(eliminate(pack_lanes([own_gram, unit])), -8)
-    alpha, rest = shift(solved, -8), shift(solved, -16)
-    beta = own_gram - product(g1, alpha) + product_t(alpha, product(g2, alpha) - g1)
-    beta = product(inverse, beta)
+    g1_cols, h1_cols = columns(g1), columns(h1)
+    alpha, rest = solve(g1_cols, [own_gram, h1])
+    alpha_t, rest_t = columns_t(alpha), columns_t(rest)
+    beta = own_gram - times(g1_cols, alpha)
+    beta = beta + times(alpha_t, times(columns(g2), alpha) - g1)
+    own_cols = columns(own_gram)
+    (beta,) = solve(own_cols, [beta])
     mix = rest + beta
-    early = product(own_gram, rest) - product(h1, alpha)
-    early = product_t(rest, early) - product_t(alpha, product(h1, rest))
+    mix_t = columns_t(mix)
+    g1_mix = times(g1_cols, mix)
+    early = times(own_cols, rest) - times(h1_cols, alpha)
+    early = times(rest_t, early) - times(alpha_t, times(h1_cols, rest))
 
     def put_table(dst, base, m):
         for i in range(N):
@@ -722,14 +726,14 @@
     lax.fori_loop(2, N, second_body, 0)
     sum2 = reduce_finish(1, 1)
 
-    h2, zs = sum2, shift(sum2, -8)
-    norm_next = early + product_t(alpha, product(h2, alpha))
-    cross = h2 + theta * h1
-    h3 = zs - theta * cross
-    curve = product_t(mix, product(g1, mix) - product(cross, alpha)) + product_t(
-        alpha, product(h3, alpha) - product(cross, mix)
+    h2_cols, zs_cols = columns(sum2), columns(sum2, 8)
+    norm_next = early + times(alpha_t, times(h2_cols, alpha))
+    cross = [h + theta * g for h, g in zip(h2_cols, h1_cols)]
+    h3_cols = [z - theta * c for z, c in zip(zs_cols, cross)]
+    curve = times(mix_t, g1_mix - times(cross, alpha)) + times(
+        alpha_t, times(h3_cols, alpha) - times(cross, mix)
     )
-    alpha2 = shift(eliminate(pack_lanes([curve, norm_next])), -8)
+    (alpha2,) = solve(columns(curve), [norm_next])
     put_table(T, 0, alpha2)
 
     for d in flat:
@@ -753,24 +757,29 @@
             for k, (buf, out) in enumerate(((X, x_out), (Y, r_out)))
         ]
 
-    for j in range(N):
-        a = [T[N * j + i] for i in range(N)]
+    for pair in range(0, N, 2):
+        js = (pair, pair + 1)
+        a = {j: [T[N * j + i] for i in range(N)] for j in js}
 
         def body(p, carry):
             for t in range(4):
                 at = pl.ds(8 * t, 8)
-                x = X1[j, p, at]
-                res = R1[j, p, at]
-                for i in range(0, N, 2):
-                    x = x + (a[i] * D2[i, p, at] + a[i + 1] * D2[i + 1, p, at])
-                    res = res - (a[i] * A2[i, p, at] + a[i + 1] * A2[i + 1, p, at])
-                X[j, p, at] = x
-                Y[j, p, at] = res
+                d = [D2[i, p, at] for i in range(N)]
+                e = [A2[i, p, at] for i in range(N)]
+                for j in js:
+                    x = X1[j, p, at]
+                    res = R1[j, p, at]
+                    for i in range(0, N, 2):
+                        x = x + (a[j][i] * d[i] + a[j][i + 1] * d[i + 1])
+                        res = res - (a[j][i] * e[i] + a[j][i + 1] * e[i + 1])
+                    X[j, p, at] = x
+                    Y[j, p, at] = res
             return carry
 
         lax.fori_loop(0, 16, body, 0)
-        for copy in store(j):
-            copy.start()
+        for j in js:
+            for copy in store(j):
+                copy.start()
     for j in range(N):
         for copy in store(j):
             copy.wait()

time: 59.1 us -> 49.7 us (0.84)
  Pallas kernels: 58.4 us -> 49 us
    pallas_call x1, Pallas kernels: 54.3 us -> 45.2 us  [shards(): pl.pallas_call(functools.partial(kernel, sizes), out_shape=(field,) * 4 +...]
where the time goes in v3:
time: 49.7 us; the launch traced here: 49.6 us
  Pallas kernels  49 us (99%)
  between operations  0.64 us (1%)
    pallas_call x1, Pallas kernels, shards(): pl.pallas_call(functools.partial(kernel, sizes), out_shape=(field,) * 4 +...  45.2 us
    pallas_call x1, Pallas kernels, shards(): pl.pallas_call(finish_kernel, out_shape=(jax.ShapeDtypeStruct(block, F32)...  3.8 us

profile of v3, /device:TPU:1, one launch (start us, length us, event | category | flops | bytes accessed | tf_op | source)
XLA Modules:
  0.0 49.6 jit_solution(7105309517564547331)
XLA Ops:
  0.6 45.2 %operator.1 = (f32[8,16,32,128]{3,2,1,0:T(8,128)S(1)}, f32[8,16,32,128]{3,2,1,0:T(8,128)S(1)}, f32[8,16,32,128]{3,2,1,0:T(8,128)S(1)}, f32[8,16,32,128]{3,2,1,0:T(8,128)S(1)}, f32[64,8,128]{2,1,0:T(8,128)S(1)}) custom-call(f32[8,16,32,128]{3,2,1,0:T(8,128)} %x_ref.1, f32[14,16,32,128]{3,2,1,0:T(8,128)} %w_ref.1), custom_call_target="tpu_custom_call" | custom-call | tf_op jit(solution)/shard_map/operator/pallas_call | solution.py:795
  45.8 3.8 %finish.1 = (f32[8,16,32,128]{3,2,1,0:T(8,128)}, f32[8,16,32,128]{3,2,1,0:T(8,128)}) custom-call(f32[8,16,32,128]{3,2,1,0:T(8,128)S(1)} %get-tuple-element.7.X1, f32[8,16,32,128]{3,2,1,0:T(8,128)S(1)} %get-tuple-element.8.R1, f32[8,16,32,128]{3,2,1,0:T(8,128)S(1)} %get-tuple-element.9.D2, f32[8,16,32,128]{3,2,1,0:T(8,128)S(1)} %get-tuple-element.10.A2, ...), custom_call_target="tpu_custom_call" | custom-call | tf_op jit(solution)/shard_map/finish/pallas_call | solution.py:831

commit v4 on v3

--- a/solution.py
+++ b/solution.py
@@ -440,15 +440,16 @@
         for lo, hi in ((0, 3), (3, N)):
             pairs = [(i, j) for i, j in PAIRS if lo <= i < hi]
 
-            def body(x, acc):
+            def body(planes, acc):
                 acc = list(acc)
-                for t in range(4):
+                for k in range(8):
+                    x, t = 2 * planes + k // 4, k % 4
                     left, right = get(x, t, range(lo, hi), range(lo, N))
                     for n, (i, j) in enumerate(pairs):
                         acc[n] = acc[n] + left[i] * right[j]
                 return tuple(acc)
 
-            sums += list(lax.fori_loop(0, 16, body, tuple(zero for _ in pairs)))
+            sums += list(lax.fori_loop(0, 8, body, tuple(zero for _ in pairs)))
         return sums
 
     def spread(parts, acc, offset):
@@ -521,32 +522,34 @@
     def operate(src, put):
         def body(x, carry):
             for t in range(4):
-                weights = [
-                    [coupling(x, t, a, b, c) for a, b in PLANE] for c in (0, 1, -1)
-                ]
                 halo = R[x, pl.ds(8 * t, 8)]
-                for f in range(N):
-                    sums = [None, None, None]
-                    for m, (a, b) in enumerate(PLANE):
-                        v = src[f, x + 1 + a, pl.ds(TOP + 8 * t + b, 8)]
-                        if (a, b) == (0, 0):
-                            centre = weights[0][m] * v
-                        for c in range(3):
-                            if c == 0 and (a, b) == (0, 0):
-                                continue
-                            term = weights[c][m] * v
-                            sums[c] = term if sums[c] is None else sums[c] + term
-                    side = shift(halo, -(2 * f + 1))
-                    total = centre - sums[0]
-                    total = total - shift(jnp.where(first, side, sums[1]), 127)
-                    total = total - shift(jnp.where(last, side, sums[2]), 1)
-                    put(f, x, t, total)
+                for group in (range(0, 4), range(4, N)):
+                    centre = {}
+                    sums = {f: [None, None, None] for f in group}
+                    for a, b in PLANE:
+                        weights = [coupling(x, t, a, b, c) for c in (0, 1, -1)]
+                        for f in group:
+                            v = src[f, x + 1 + a, pl.ds(TOP + 8 * t + b, 8)]
+                            for c in range(3):
+                                term = weights[c] * v
+                                if c == 0 and (a, b) == (0, 0):
+                                    centre[f] = term
+                                elif sums[f][c] is None:
+                                    sums[f][c] = term
+                                else:
+                                    sums[f][c] = sums[f][c] + term
+                    for f in group:
+                        side = shift(halo, -(2 * f + 1))
+                        total = centre[f] - sums[f][0]
+                        total = total - shift(jnp.where(first, side, sums[f][1]), 127)
+                        total = total - shift(jnp.where(last, side, sums[f][2]), 1)
+                        put(f, x, t, total)
             return carry
 
         return body
 
     def ends(body):
-        return lambda i, carry: body(15 * i, carry)
+        lax.fori_loop(0, 2, lambda i, carry: body(15 * i, carry), 0)
 
     def put_q(f, x, t, value):
         Q[f, x + 1, pl.ds(TOP + 8 * t, 8)] = value
@@ -555,8 +558,8 @@
         S[f, x, pl.ds(8 * t, 8)] = value
 
     blocks(prepare, 1, 5, 3)
-    lax.fori_loop(1, 15, edges, 0)
-    lax.fori_loop(1, 15, operate(V, put_q), 0)
+    blocks(edges, 1, 7, 2)
+    blocks(operate(V, put_q), 1, 14, 1)
     for d in flat_x:
         recv_if(d, field_part(d, V, send1, recv1))
     for d in flat_wx:
@@ -566,8 +569,8 @@
     unpack(get_lpp(0), G, (0, 17))
     unpack(get_lpp(1), GW, (0,))
     prepare(0, 0)
-    lax.fori_loop(0, 2, ends(edges), 0)
-    lax.fori_loop(0, 2, ends(operate(V, put_q)), 0)
+    ends(edges)
+    ends(operate(V, put_q))
 
     for d in flat_y + flat_x:
         start_if(d, field_part(d, Q, send2, recv2))
@@ -629,17 +632,17 @@
     for d in cols_y:
         recv_if(d, column_part(d, False))
     unpack(get_lpq, G, range(1, 17))
-    lax.fori_loop(1, 15, edges, 0)
-    lax.fori_loop(1, 5, operate(Q, put_s), 0)
+    blocks(edges, 1, 7, 2)
+    blocks(operate(Q, put_s), 1, 4, 1)
     reduce_start(0, 1, reduce_finish(0, 0))
-    lax.fori_loop(5, 15, operate(Q, put_s), 0)
+    blocks(operate(Q, put_s), 5, 10, 1)
     for d in flat_x:
         recv_if(d, field_part(d, Q, send2, recv2))
     for d in cols_x:
         recv_if(d, column_part(d, False))
     unpack(get_lpq, G, (0, 17))
-    lax.fori_loop(0, 2, ends(edges), 0)
-    lax.fori_loop(0, 2, ends(operate(Q, put_s)), 0)
+    ends(edges)
+    ends(operate(Q, put_s))
     sum1 = reduce_finish(0, 1)
 
     def trace(m):
@@ -724,6 +727,16 @@
     lax.fori_loop(0, 2, second_body, 0)
     reduce_start(1, 1, reduce_finish(1, 0))
     lax.fori_loop(2, N, second_body, 0)
+    for d in flat:
+        sent_if(d, field_part(d, V, send1, recv1))
+        sent_if(d, field_part(d, Q, send2, recv2))
+    for d in flat_w:
+        sent_if(d, weight_part(d))
+    for d in cols:
+        sent_if(d, column_part(d, True))
+        sent_if(d, column_part(d, False))
+    for copy in reduce_copies(0, 0) + reduce_copies(0, 1):
+        copy.wait_send()
     sum2 = reduce_finish(1, 1)
 
     h2_cols, zs_cols = columns(sum2), columns(sum2, 8)
@@ -736,34 +749,29 @@
     (alpha2,) = solve(columns(curve), [norm_next])
     put_table(T, 0, alpha2)
 
-    for d in flat:
-        sent_if(d, field_part(d, V, send1, recv1))
-        sent_if(d, field_part(d, Q, send2, recv2))
-    for d in flat_w:
-        sent_if(d, weight_part(d))
-    for d in cols:
-        sent_if(d, column_part(d, True))
-        sent_if(d, column_part(d, False))
-    for which in range(2):
-        for step in range(2):
-            for copy in reduce_copies(which, step):
-                copy.wait_send()
+    for copy in reduce_copies(1, 0) + reduce_copies(1, 1):
+        copy.wait_send()
 
 
 def finish_kernel(X1, R1, D2, A2, T, x_out, r_out, X, Y, sems):
-    def store(j):
+    def store(j, lo, count):
+        at = pl.ds(lo, count)
         return [
-            pltpu.make_async_copy(buf.at[j], out.at[j], sems.at[k, j])
+            pltpu.make_async_copy(
+                buf.at[j, at], out.at[j, at], sems.at[k, j + lo // 4]
+            )
             for k, (buf, out) in enumerate(((X, x_out), (Y, r_out)))
         ]
 
+    started = []
     for pair in range(0, N, 2):
         js = (pair, pair + 1)
         a = {j: [T[N * j + i] for i in range(N)] for j in js}
 
-        def body(p, carry):
-            for t in range(4):
-                at = pl.ds(8 * t, 8)
+        def body(planes, carry):
+            for k in range(8):
+                p = 2 * planes + k // 4
+                at = pl.ds(8 * (k % 4), 8)
                 d = [D2[i, p, at] for i in range(N)]
                 e = [A2[i, p, at] for i in range(N)]
                 for j in js:
@@ -776,13 +784,14 @@
                     Y[j, p, at] = res
             return carry
 
-        lax.fori_loop(0, 16, body, 0)
-        for j in js:
-            for copy in store(j):
-                copy.start()
-    for j in range(N):
-        for copy in store(j):
-            copy.wait()
+        for lo, count in ((0, 16),) if pair < 6 else ((0, 8), (8, 8)):
+            lax.fori_loop(lo // 2, (lo + count) // 2, body, 0)
+            for j in js:
+                for copy in store(j, lo, count):
+                    copy.start()
+                    started.append(copy)
+    for copy in started:
+        copy.wait()
 
 
 def shards(sizes, rhs, stencil):
@@ -836,7 +845,7 @@
         scratch_shapes=[
             pltpu.VMEM(block, F32),
             pltpu.VMEM(block, F32),
-            pltpu.SemaphoreType.DMA((2, N)),
+            pltpu.SemaphoreType.DMA((2, N + 2)),
         ],
         compiler_params=pltpu.CompilerParams(vmem_limit_bytes=24 * 2**20),
         name="finish",

time: 49.7 us -> 48.6 us (0.978)
  Pallas kernels: 49 us -> 47.8 us
    pallas_call x1, Pallas kernels: 45.2 us -> 44.4 us  [shards(): pl.pallas_call(functools.partial(kernel, sizes), out_shape=(field,) * 4 +...]
where the time goes in v4:
time: 48.6 us; the launch traced here: 48.5 us
  Pallas kernels  47.8 us (98%)
  between operations  0.64 us (1%)
    pallas_call x1, Pallas kernels, shards(): pl.pallas_call(functools.partial(kernel, sizes), out_shape=(field,) * 4 +...  44.4 us
    pallas_call x1, Pallas kernels, shards(): pl.pallas_call(finish_kernel, out_shape=(jax.ShapeDtypeStruct(block, F32)...  3.4 us

profile of v4, /device:TPU:1, one launch (start us, length us, event | category | flops | bytes accessed | tf_op | source)
XLA Modules:
  0.0 48.5 jit_solution(7022719473406656736)
XLA Ops:
  0.6 44.4 %operator.1 = (f32[8,16,32,128]{3,2,1,0:T(8,128)S(1)}, f32[8,16,32,128]{3,2,1,0:T(8,128)S(1)}, f32[8,16,32,128]{3,2,1,0:T(8,128)S(1)}, f32[8,16,32,128]{3,2,1,0:T(8,128)S(1)}, f32[64,8,128]{2,1,0:T(8,128)S(1)}) custom-call(f32[8,16,32,128]{3,2,1,0:T(8,128)} %x_ref.1, f32[14,16,32,128]{3,2,1,0:T(8,128)} %w_ref.1), custom_call_target="tpu_custom_call" | custom-call | tf_op jit(solution)/shard_map/operator/pallas_call | solution.py:804
  45.1 3.4 %finish.1 = (f32[8,16,32,128]{3,2,1,0:T(8,128)}, f32[8,16,32,128]{3,2,1,0:T(8,128)}) custom-call(f32[8,16,32,128]{3,2,1,0:T(8,128)S(1)} %get-tuple-element.7.X1, f32[8,16,32,128]{3,2,1,0:T(8,128)S(1)} %get-tuple-element.8.R1, f32[8,16,32,128]{3,2,1,0:T(8,128)S(1)} %get-tuple-element.9.D2, f32[8,16,32,128]{3,2,1,0:T(8,128)S(1)} %get-tuple-element.10.A2, ...), custom_call_target="tpu_custom_call" | custom-call | tf_op jit(solution)/shard_map/finish/pallas_call | solution.py:840

commit v5 on v4

--- a/solution.py
+++ b/solution.py
@@ -624,8 +624,8 @@
         return q, q
 
     parts1 = spread(parts1, gram_loop(get_rq), 8)
-    parts1 = spread(parts1, gram_loop(get_qq), 16)
     reduce_start(0, 0, fold(parts1))
+    reduce_start(2, 0, fold(spread([zero] * N, gram_loop(get_qq), 0)))
 
     for d in flat_y:
         recv_if(d, field_part(d, Q, send2, recv2))
@@ -635,6 +635,7 @@
     blocks(edges, 1, 7, 2)
     blocks(operate(Q, put_s), 1, 4, 1)
     reduce_start(0, 1, reduce_finish(0, 0))
+    reduce_start(2, 1, reduce_finish(2, 0))
     blocks(operate(Q, put_s), 5, 10, 1)
     for d in flat_x:
         recv_if(d, field_part(d, Q, send2, recv2))
@@ -652,7 +653,6 @@
     small = lane < 8
     own_gram = jnp.where(small, sum1, 0.0)
     g1 = jnp.where(small, shift(sum1, -8), 0.0)
-    g2 = shift(sum1, -16)
     theta = trace(g1) / trace(own_gram)
     h1 = g1 - theta * own_gram
 
@@ -675,6 +675,7 @@
     reduce_start(1, 0, fold(parts2))
 
     unit = jnp.where(lane == rows(), 1.0, 0.0)
+    g2 = reduce_finish(2, 1)
     g1_cols, h1_cols = columns(g1), columns(h1)
     alpha, rest = solve(g1_cols, [own_gram, h1])
     alpha_t, rest_t = columns_t(alpha), columns_t(rest)
@@ -735,8 +736,9 @@
     for d in cols:
         sent_if(d, column_part(d, True))
         sent_if(d, column_part(d, False))
-    for copy in reduce_copies(0, 0) + reduce_copies(0, 1):
-        copy.wait_send()
+    for which in (0, 2):
+        for copy in reduce_copies(which, 0) + reduce_copies(which, 1):
+            copy.wait_send()
     sum2 = reduce_finish(1, 1)
 
     h2_cols, zs_cols = columns(sum2), columns(sum2, 8)
@@ -822,15 +824,15 @@
             pltpu.VMEM((2, 4, 48, 128), F32),
             pltpu.VMEM((18, 48, 128), F32),
             pltpu.VMEM((17, 48, 128), F32),
-            pltpu.VMEM((2, 2, 8, 128), F32),
-            pltpu.VMEM((2, ny + nx * nz, 8, 128), F32),
+            pltpu.VMEM((3, 2, 8, 128), F32),
+            pltpu.VMEM((3, ny + nx * nz, 8, 128), F32),
             pltpu.SemaphoreType.DMA((2,)),
             pltpu.SemaphoreType.DMA((31,)),
             pltpu.SemaphoreType.DMA((31,)),
             pltpu.SemaphoreType.DMA((26,)),
             pltpu.SemaphoreType.DMA((26,)),
-            pltpu.SemaphoreType.DMA((2, ny + nx * nz)),
-            pltpu.SemaphoreType.DMA((2, ny + nx * nz)),
+            pltpu.SemaphoreType.DMA((3, ny + nx * nz)),
+            pltpu.SemaphoreType.DMA((3, ny + nx * nz)),
         ],
         compiler_params=pltpu.CompilerParams(
             collective_id=0, has_side_effects=True, vmem_limit_bytes=44 * 2**20

time: 48.6 us -> 48.4 us (level)
  no operation moved by 1% of the time
where the time goes in v5:
time: 48.4 us; the launch traced here: 48.3 us
  Pallas kernels  47.7 us (99%)
  between operations  0.64 us (1%)
    pallas_call x1, Pallas kernels, shards(): pl.pallas_call(functools.partial(kernel, sizes), out_shape=(field,) * 4 +...  44.3 us
    pallas_call x1, Pallas kernels, shards(): pl.pallas_call(finish_kernel, out_shape=(jax.ShapeDtypeStruct(block, F32)...  3.4 us

profile of v5, /device:TPU:1, one launch (start us, length us, event | category | flops | bytes accessed | tf_op | source)
XLA Modules:
  0.0 48.3 jit_solution(17959180683911908102)
XLA Ops:
  0.6 44.3 %operator.1 = (f32[8,16,32,128]{3,2,1,0:T(8,128)S(1)}, f32[8,16,32,128]{3,2,1,0:T(8,128)S(1)}, f32[8,16,32,128]{3,2,1,0:T(8,128)S(1)}, f32[8,16,32,128]{3,2,1,0:T(8,128)S(1)}, f32[64,8,128]{2,1,0:T(8,128)S(1)}) custom-call(f32[8,16,32,128]{3,2,1,0:T(8,128)} %x_ref.1, f32[14,16,32,128]{3,2,1,0:T(8,128)} %w_ref.1), custom_call_target="tpu_custom_call" | custom-call | tf_op jit(solution)/shard_map/operator/pallas_call | solution.py:806
  44.9 3.4 %finish.1 = (f32[8,16,32,128]{3,2,1,0:T(8,128)}, f32[8,16,32,128]{3,2,1,0:T(8,128)}) custom-call(f32[8,16,32,128]{3,2,1,0:T(8,128)S(1)} %get-tuple-element.7.X1, f32[8,16,32,128]{3,2,1,0:T(8,128)S(1)} %get-tuple-element.8.R1, f32[8,16,32,128]{3,2,1,0:T(8,128)S(1)} %get-tuple-element.9.D2, f32[8,16,32,128]{3,2,1,0:T(8,128)S(1)} %get-tuple-element.10.A2, ...), custom_call_target="tpu_custom_call" | custom-call | tf_op jit(solution)/shard_map/finish/pallas_call | solution.py:842
